TPU v7x, 32 devices: a whole 2x2x4 slice. The times are simulated.
32 devices in a mesh: dp: 4 (over z), sx: 4 (over y, core), sy: 2 (over x).
Axes of the slice: x: 2, y: 2, z: 4, core: 2. Of those that a mesh axis runs over, the one named last changes fastest.
Arguments:
- volume: bfloat16 [4, 4, 16, 16, 128], P('dp', None, 'sx', 'sy'), may hold values from -6 to 6
- first_weight: bfloat16 [32, 108], replicated, may hold values from -0.625 to 0.625
- second_weight: bfloat16 [64, 864], replicated, may hold values from -0.21875 to 0.21875
- cotangent: bfloat16 [4, 64, 8, 8, 64], P('dp', None, 'sx', 'sy'), may hold values from -6 to 6
Outputs:
- grad_first: float32 [32, 108], replicated
- grad_second: float32 [64, 864], replicated
All inputs are finite; a program needn't handle non-finite values.
Results may differ from a plain program's by a relative error of at most 0.014.
Values may be sent and summed in bfloat16 or wider, within the bound.
No kernel may reach another device: no remote copies, remote signals or barrier semaphores. Data moves between devices by JAX's collectives and lax.ppermute only.
A program may use at most 64 MiB of HBM per device.

v0:
```python
import jax
import jax.numpy as jnp
from jax import lax
from jax.sharding import PartitionSpec as P


def padded_2(block, sides, width):
    for axis, dim in sides:
        count = lax.axis_size(axis)
        forward = [(i, i + 1) for i in range(count - 1)]
        backward = [(target, source) for source, target in forward]
        low = lax.ppermute(
            lax.slice_in_dim(block, block.shape[dim] - width, None, axis=dim), axis, forward
        )
        high = lax.ppermute(lax.slice_in_dim(block, 0, width, axis=dim), axis, backward)
        block = jnp.concatenate([low, block, high], axis=dim)
    return block


def leaky(value):
    return 0.3 * value + 0.7 * jax.nn.softplus(value)


def slope(value):
    return 0.3 + 0.7 * jax.nn.sigmoid(value)


def patches(padded, width_x, width_y, width_z):
    columns = []
    for shift_x in range(3):
        for shift_y in range(3):
            for shift_z in range(3):
                columns.append(
                    padded[
                        :,
                        shift_x : shift_x + width_x,
                        shift_y : shift_y + width_y,
                        shift_z : shift_z + width_z,
                    ]
                )
    stacked = jnp.concatenate(columns, 0)
    return stacked.reshape(stacked.shape[0], width_x * width_y * width_z)


def pad_depth(field):
    return jnp.pad(field, ((0, 0), (0, 0), (0, 0), (1, 1)))


def shards(volume, first_weight, second_weight, cotangent):
    sample = volume[0]
    chans, width_x, width_y, width_z = sample.shape
    devices = lax.axis_size("dp") * lax.axis_size("sx") * lax.axis_size("sy")
    fine_rim = padded_2(sample, (("sx", 1), ("sy", 2)), 1)
    fine_cols = patches(pad_depth(fine_rim), width_x, width_y, width_z)
    pre_first = jnp.dot(first_weight, fine_cols, preferred_element_type=jnp.float32)
    hidden = leaky(pre_first).astype(jnp.bfloat16)
    inner = hidden.shape[0]
    half_x, half_y, half_z = (width_x // 2, width_y // 2, width_z // 2)
    pooled = (
        hidden.astype(jnp.float32)
        .reshape(inner, half_x, 2, half_y, 2, half_z, 2)
        .sum(axis=(2, 4, 6))
        * 0.125
    ).astype(jnp.bfloat16)
    pooled_rim = padded_2(pooled, (("sx", 1), ("sy", 2)), 1)
    coarse_cols = patches(pad_depth(pooled_rim), half_x, half_y, half_z)
    pre_second = jnp.dot(second_weight, coarse_cols, preferred_element_type=jnp.float32)
    outer = pre_second.shape[0]
    back = (cotangent[0].reshape(outer, -1).astype(jnp.float32) * slope(pre_second)).astype(
        jnp.bfloat16
    )
    coarse_count = half_x * half_y * half_z * devices
    scale_second = 1.0 / jnp.sqrt(jnp.float32(coarse_count))
    scale_first = 1.0 / jnp.sqrt(jnp.float32(coarse_count * 8))
    grad_second = (
        lax.dot_general(
            back, coarse_cols, (((1,), (1,)), ((), ())), preferred_element_type=jnp.float32
        )
        * scale_second
    )
    back_rim = padded_2(back.reshape(outer, half_x, half_y, half_z), (("sx", 1), ("sy", 2)), 1)
    back_cols = patches(pad_depth(back_rim), half_x, half_y, half_z)
    mirrored = (
        second_weight.reshape(outer, 27, inner)[:, ::-1, :]
        .transpose(2, 1, 0)
        .reshape(inner, 27 * outer)
    )
    up = jnp.dot(mirrored, back_cols, preferred_element_type=jnp.float32)
    spread = jnp.broadcast_to(
        up.reshape(inner, half_x, 1, half_y, 1, half_z, 1), (inner, half_x, 2, half_y, 2, half_z, 2)
    ).reshape(inner, -1)
    lower = (spread * 0.125 * slope(pre_first)).astype(jnp.bfloat16)
    grad_first = (
        lax.dot_general(
            lower, fine_cols, (((1,), (1,)), ((), ())), preferred_element_type=jnp.float32
        )
        * scale_first
    )
    shared = (
        lax.psum_scatter(
            grad_first.astype(jnp.bfloat16), ("sx", "sy"), scatter_dimension=0, tiled=True
        ).astype(jnp.float32),
        lax.psum_scatter(
            grad_second.astype(jnp.bfloat16), ("sx", "sy"), scatter_dimension=0, tiled=True
        ).astype(jnp.float32),
    )
    shared = lax.psum((shared[0], shared[1]), "dp")
    grad_first, grad_second = (
        lax.all_gather(shared[0], ("sx", "sy"), axis=0, tiled=True),
        lax.all_gather(shared[1], ("sx", "sy"), axis=0, tiled=True),
    )
    return (grad_first, grad_second)


def solution(mesh):
    return jax.shard_map(
        shards,
        mesh=mesh,
        in_specs=(P("dp", None, "sx", "sy", None), P(), P(), P("dp", None, "sx", "sy", None)),
        out_specs=(P(), P()),
        check_vma=False,
    )
```

profile of v0, /device:TPU:0, one launch (start us, length us, event | category | flops | bytes accessed | tf_op | source)
XLA Modules:
  0.0 207.3 jit_solution(6749969575583011790)
XLA Ops:
  8.0 2.4 %collective-permute-start = (bf16[4,1,8,128]{3,2,1,0:T(8,128)(2,1)S(1)}, bf16[4,1,8,128]{3,2,1,0:T(8,128)(2,1)S(1)}, u32[]{:S(2)}, u32[]{:S(2)}) collective-permute-start(bf16[4,1,8,128]{3,2,1,0:T(8,128)(2,1)S(1)} %get-tuple-element.100), channel_id=1, source_target_pairs={{0,2},{2,4},{4,6},{1,3},{3,5},{5,7},{8,10},{10,12},{12,14},{9,11},... | collective-permute-start | bytes 24584 | tf_op jit(solution)/shard_map/ppermute | solution.py:12
  10.3 1.3 collective-permute-start.1
  11.6 0.8 concatenate.201
  12.4 1.1 copy.12
  13.5 2.0 collective-permute-done.1
  15.5 0.9 pad_maximum_fusion.19
  16.4 3.4 %collective-permute-start.2 = (bf16[4,6,1,128]{3,2,1,0:T(2,128)(2,1)S(1)}, bf16[4,6,1,128]{3,2,1,0:T(2,128)(2,1)S(1)}, u32[]{:S(2)}, u32[]{:S(2)}) collective-permute-start(bf16[4,6,1,128]{3,2,1,0:T(2,128)(2,1)S(1)} %get-tuple-element.96), channel_id=1, source_target_pairs={{0,1},{2,3},{4,5},{6,7},{8,9},{10,11},{12,13},{14,15},{16,17},{18,... | collective-permute-start | bytes 18440 | tf_op jit(solution)/shard_map/ppermute | solution.py:12
  19.8 1.3 collective-permute-start.3
  21.1 0.8 fusion.36
  22.0 3.4 %collective-permute-done.3 = bf16[4,6,1,128]{3,2,1,0:T(2,128)(2,1)S(1)} collective-permute-done((bf16[4,6,1,128]{3,2,1,0:T(2,128)(2,1)S(1)}, bf16[4,6,1,128]{3,2,1,0:T(2,128)(2,1)S(1)}, u32[]{:S(2)}, u32[]{:S(2)}) %collective-permute-start.3) | collective-permute-done | bytes 6176 | tf_op jit(solution)/shard_map/ppermute | solution.py:15
  25.4 0.9 pad_maximum_fusion.11
  27.9 1.4 fusion.27
  29.3 1.6 copy.11
  31.0 1.3 reduce_sum.9
  32.4 2.9 %collective-permute-start.4 = (bf16[32,1,4,64]{0,3,2,1:T(8,128)(2,1)S(1)}, bf16[32,1,4,64]{0,3,2,1:T(8,128)(2,1)S(1)}, u32[]{:S(2)}, u32[]{:S(2)}) collective-permute-start(bf16[32,1,4,64]{0,3,2,1:T(8,128)(2,1)S(1)} %get-tuple-element.86), channel_id=1, source_target_pairs={{0,2},{2,4},{4,6},{1,3},{3,5},{5,7},{8,10},{10,12},{12,14},{9,11},... | collective-permute-start | bytes 49160 | tf_op jit(solution)/shard_map/ppermute | solution.py:12
  35.3 1.3 collective-permute-start.5
  38.5 1.7 reshape.95
  40.3 0.9 reshape.94
  41.2 2.0 collective-permute-start.6
  43.2 1.3 collective-permute-start.7
  45.3 4.1 %collective-permute-done.7 = bf16[32,4,1,64]{0,3,2,1:T(8,128)(2,1)S(1)} collective-permute-done((bf16[32,4,1,64]{0,3,2,1:T(8,128)(2,1)S(1)}, bf16[32,4,1,64]{0,3,2,1:T(8,128)(2,1)S(1)}, u32[]{:S(2)}, u32[]{:S(2)}) %collective-permute-start.7) | collective-permute-done | bytes 16416 | tf_op jit(solution)/shard_map/ppermute | solution.py:15
  49.5 0.8 fusion.43
  50.3 0.8 fusion.44
  51.3 1.1 fusion.42
  52.4 4.9 %concatenate.223 = bf16[864,2,4,64]{0,3,2,1:T(8,128)(2,1)S(1)} concatenate(bf16[32,2,4,64]{0,3,2,1:T(8,128)(2,1)} %get-tuple-element.39, bf16[32,2,4,64]{0,3,2,1:T(8,128)(2,1)} %get-tuple-element.51, bf16[32,2,4,64]{0,3,2,1:T(8,128)(2,1)} %get-tuple-element.38, bf16[32,2,4,64]{0,3,2,1:T(8,128)(2,1)} %get-tuple-element.37, bf16[32,2,4,64]{0,3,2,1:T(8,128)(2,1)} %get-tuple-element.85, ...), dimensions={0} | concatenate | bytes 1769472 | tf_op jit(solution)/shard_map/concatenate | solution.py:41
  57.3 1.4 fusion.8
  58.9 2.7 %collective-permute-start.8 = (bf16[64,1,4,64]{3,2,1,0:T(4,128)(2,1)S(1)}, bf16[64,1,4,64]{3,2,1,0:T(4,128)(2,1)S(1)}, u32[]{:S(2)}, u32[]{:S(2)}) collective-permute-start(bf16[64,1,4,64]{3,2,1,0:T(4,128)(2,1)S(1)} %get-tuple-element.83), channel_id=1, source_target_pairs={{0,2},{2,4},{4,6},{1,3},{3,5},{5,7},{8,10},{10,12},{12,14},{9,11},... | collective-permute-start | bytes 98312 | tf_op jit(solution)/shard_map/ppermute | solution.py:12
  61.6 0.9 fusion
  62.6 1.3 collective-permute-start.9
  63.9 4.5 %collective-permute-done.9 = bf16[64,1,4,64]{3,2,1,0:T(4,128)(2,1)S(1)} collective-permute-done((bf16[64,1,4,64]{3,2,1,0:T(4,128)(2,1)S(1)}, bf16[64,1,4,64]{3,2,1,0:T(4,128)(2,1)S(1)}, u32[]{:S(2)}, u32[]{:S(2)}) %collective-permute-start.9) | collective-permute-done | bytes 32800 | tf_op jit(solution)/shard_map/ppermute | solution.py:15
  69.0 0.8 concatenate.232
  69.8 1.6 collective-permute-start.10
  71.4 1.5 collective-permute-start.11
  72.8 44.2 %all-reduce.8.cloned.1.call-done = bf16[64,864]{1,0:T(8,128)(2,1)} async-done(((bf16[64,864]{1,0:T(8,128)(2,1)}), bf16[64,864]{1,0:T(8,128)(2,1)}) %all-reduce.8.cloned.1.call-update) | async-done | bytes 110608
  117.8 1.1 pad_maximum_fusion.1
  119.8 0.8 concatenate.244
  120.5 0.8 concatenate.228
  122.8 0.9 fusion.17
  123.7 1.1 fusion.41
  124.9 0.8 concatenate.255
  128.8 0.9 constant_dynamic-update-slice_fusion.28
  130.7 1.0 broadcast_in_dim.2
  131.7 1.4 copy.15
  133.1 1.6 fusion.10
  134.7 14.5 %all-reduce.3 = bf16[32,108]{1,0:T(8,128)(2,1)S(1)} all-reduce(bf16[32,108]{1,0:T(8,128)(2,1)S(1)} %fusion.10), channel_id=2, replica_groups=mesh['dp'=4,'sx'=4,'sy'=2] {'sx','sy'}, use_global_device_ids=true, to_apply=%region_1.2.clone | all-reduce | flops 3456 | bytes 13824
  149.2 19.0 %all-reduce.5 = (f32[4,108]{1,0:T(4,128)S(1)}, f32[8,864]{1,0:T(8,128)S(1)}) all-reduce(f32[4,108]{1,0:T(4,128)S(1)} %dynamic-slice_convert_fusion.1, f32[8,864]{1,0:T(8,128)S(1)} %dynamic-slice_convert_fusion), channel_id=1, replica_groups=mesh['dp'=4,'sx'=4,'sy'=2] {'dp'}, use_global_device_ids=true, to_apply=%region_2.3 | all-reduce | flops 7344 | bytes 58752 | tf_op jit(solution)/shard_map/psum | solution.py:107
  168.2 14.8 %all-gather = f32[8,4,108]{2,1,0:T(4,128)S(1)} all-gather(f32[1,4,108]{2,1,0:T(4,128)S(1)} %bitcast.186), channel_id=1, replica_groups=mesh['dp'=4,'sx'=4,'sy'=2] {'sx','sy'}, dimensions={0}, use_global_device_ids=true | all-gather | bytes 15552 | tf_op jit(solution)/shard_map/all_gather | solution.py:109
  183.0 16.1 %all_gather.7 = f32[64,864]{1,0:T(8,128)S(1)} all-gather(f32[8,864]{1,0:T(8,128)S(1)} %get-tuple-element.3), channel_id=1, replica_groups=mesh['dp'=4,'sx'=4,'sy'=2] {'sx','sy'}, dimensions={0}, use_global_device_ids=true | all-gather | bytes 248832 | tf_op jit(solution)/shard_map/all_gather | solution.py:110
  (122 shorter events, 13.2 us)
Async XLA Ops:
  7.2 20.8 %copy-start = (bf16[32,108]{1,0:T(8,128)(2,1)S(1)}, bf16[32,108]{1,0:T(8,128)(2,1)}, u32[]{:S(2)}) copy-start(bf16[32,108]{1,0:T(8,128)(2,1)} %param.5) | copy-start | bytes 20740
  7.2 19.3 %copy-start.1 = (bf16[1,4,4,8,128]{4,3,2,1,0:T(8,128)(2,1)S(1)}, bf16[1,4,4,8,128]{4,3,2,1,0:T(8,128)(2,1)}, u32[]{:S(2)}) copy-start(bf16[1,4,4,8,128]{4,3,2,1,0:T(8,128)(2,1)} %param.4) | copy-start | bytes 98308
  7.2 109.9 %all-reduce.8.cloned.1.call-start = ((), (), s32[]{:S(2)}) async-start(), calls=%async_computation | async-start | bytes 229376
  8.0 5.5 %collective-permute-start = (bf16[4,1,8,128]{3,2,1,0:T(8,128)(2,1)S(1)}, bf16[4,1,8,128]{3,2,1,0:T(8,128)(2,1)S(1)}, u32[]{:S(2)}, u32[]{:S(2)}) collective-permute-start(bf16[4,1,8,128]{3,2,1,0:T(8,128)(2,1)S(1)} %get-tuple-element.100), channel_id=1, source_target_pairs={{0,2},{2,4},{4,6},{1,3},{3,5},{5,7},{8,10},{10,12},{12,14},{9,11},... | collective-permute-start | bytes 24584 | tf_op jit(solution)/shard_map/ppermute | solution.py:12
  10.3 5.2 %collective-permute-start.1 = (bf16[4,1,8,128]{3,2,1,0:T(8,128)(2,1)S(1)}, bf16[4,1,8,128]{3,2,1,0:T(8,128)(2,1)S(1)}, u32[]{:S(2)}, u32[]{:S(2)}) collective-permute-start(bf16[4,1,8,128]{3,2,1,0:T(8,128)(2,1)S(1)} %get-tuple-element.101), channel_id=1, source_target_pairs={{2,0},{4,2},{6,4},{3,1},{5,3},{7,5},{10,8},{12,10},{14,12},{11,9},... | collective-permute-start | bytes 24584 | tf_op jit(solution)/shard_map/ppermute | solution.py:15
  16.4 5.6 %collective-permute-start.2 = (bf16[4,6,1,128]{3,2,1,0:T(2,128)(2,1)S(1)}, bf16[4,6,1,128]{3,2,1,0:T(2,128)(2,1)S(1)}, u32[]{:S(2)}, u32[]{:S(2)}) collective-permute-start(bf16[4,6,1,128]{3,2,1,0:T(2,128)(2,1)S(1)} %get-tuple-element.96), channel_id=1, source_target_pairs={{0,1},{2,3},{4,5},{6,7},{8,9},{10,11},{12,13},{14,15},{16,17},{18,... | collective-permute-start | bytes 18440 | tf_op jit(solution)/shard_map/ppermute | solution.py:12
  19.8 5.6 %collective-permute-start.3 = (bf16[4,6,1,128]{3,2,1,0:T(2,128)(2,1)S(1)}, bf16[4,6,1,128]{3,2,1,0:T(2,128)(2,1)S(1)}, u32[]{:S(2)}, u32[]{:S(2)}) collective-permute-start(bf16[4,6,1,128]{3,2,1,0:T(2,128)(2,1)S(1)} %get-tuple-element.97), channel_id=1, source_target_pairs={{1,0},{3,2},{5,4},{7,6},{9,8},{11,10},{13,12},{15,14},{17,16},{19,... | collective-permute-start | bytes 18440 | tf_op jit(solution)/shard_map/ppermute | solution.py:15
  31.0 5.6 %copy-start.10 = (u32[32]{0:T(128)S(1)}, u32[32]{0:T(128)}, u32[]{:S(2)}) copy-start(u32[32]{0:T(128)} %constant.33) | copy-start | bytes 388
  32.4 8.8 %collective-permute-start.4 = (bf16[32,1,4,64]{0,3,2,1:T(8,128)(2,1)S(1)}, bf16[32,1,4,64]{0,3,2,1:T(8,128)(2,1)S(1)}, u32[]{:S(2)}, u32[]{:S(2)}) collective-permute-start(bf16[32,1,4,64]{0,3,2,1:T(8,128)(2,1)S(1)} %get-tuple-element.86), channel_id=1, source_target_pairs={{0,2},{2,4},{4,6},{1,3},{3,5},{5,7},{8,10},{10,12},{12,14},{9,11},... | collective-permute-start | bytes 49160 | tf_op jit(solution)/shard_map/ppermute | solution.py:12
  35.3 5.9 %collective-permute-start.5 = (bf16[32,1,4,64]{0,3,2,1:T(8,128)(2,1)S(1)}, bf16[32,1,4,64]{0,3,2,1:T(8,128)(2,1)S(1)}, u32[]{:S(2)}, u32[]{:S(2)}) collective-permute-start(bf16[32,1,4,64]{0,3,2,1:T(8,128)(2,1)S(1)} %get-tuple-element.87), channel_id=1, source_target_pairs={{2,0},{4,2},{6,4},{3,1},{5,3},{7,5},{10,8},{12,10},{14,12},{11,9},... | collective-permute-start | bytes 49160 | tf_op jit(solution)/shard_map/ppermute | solution.py:15
  41.2 4.1 %collective-permute-start.6 = (bf16[32,4,1,64]{0,3,2,1:T(8,128)(2,1)S(1)}, bf16[32,4,1,64]{0,3,2,1:T(8,128)(2,1)S(1)}, u32[]{:S(2)}, u32[]{:S(2)}) collective-permute-start(bf16[32,4,1,64]{0,3,2,1:T(8,128)(2,1)S(1)} %get-tuple-element.59), channel_id=1, source_target_pairs={{0,1},{2,3},{4,5},{6,7},{8,9},{10,11},{12,13},{14,15},{16,17},{18,... | collective-permute-start | bytes 49160 | tf_op jit(solution)/shard_map/ppermute | solution.py:12
  43.2 6.2 %collective-permute-start.7 = (bf16[32,4,1,64]{0,3,2,1:T(8,128)(2,1)S(1)}, bf16[32,4,1,64]{0,3,2,1:T(8,128)(2,1)S(1)}, u32[]{:S(2)}, u32[]{:S(2)}) collective-permute-start(bf16[32,4,1,64]{0,3,2,1:T(8,128)(2,1)S(1)} %get-tuple-element.60), channel_id=1, source_target_pairs={{1,0},{3,2},{5,4},{7,6},{9,8},{11,10},{13,12},{15,14},{17,16},{19,... | collective-permute-start | bytes 49160 | tf_op jit(solution)/shard_map/ppermute | solution.py:15
  58.9 5.0 %collective-permute-start.8 = (bf16[64,1,4,64]{3,2,1,0:T(4,128)(2,1)S(1)}, bf16[64,1,4,64]{3,2,1,0:T(4,128)(2,1)S(1)}, u32[]{:S(2)}, u32[]{:S(2)}) collective-permute-start(bf16[64,1,4,64]{3,2,1,0:T(4,128)(2,1)S(1)} %get-tuple-element.83), channel_id=1, source_target_pairs={{0,2},{2,4},{4,6},{1,3},{3,5},{5,7},{8,10},{10,12},{12,14},{9,11},... | collective-permute-start | bytes 98312 | tf_op jit(solution)/shard_map/ppermute | solution.py:12
  62.6 5.8 %collective-permute-start.9 = (bf16[64,1,4,64]{3,2,1,0:T(4,128)(2,1)S(1)}, bf16[64,1,4,64]{3,2,1,0:T(4,128)(2,1)S(1)}, u32[]{:S(2)}, u32[]{:S(2)}) collective-permute-start(bf16[64,1,4,64]{3,2,1,0:T(4,128)(2,1)S(1)} %get-tuple-element.82), channel_id=1, source_target_pairs={{2,0},{4,2},{6,4},{3,1},{5,3},{7,5},{10,8},{12,10},{14,12},{11,9},... | collective-permute-start | bytes 98312 | tf_op jit(solution)/shard_map/ppermute | solution.py:15
  69.8 48.0 %collective-permute-start.10 = (bf16[64,4,1,64]{3,2,1,0:T(2,128)(2,1)S(1)}, bf16[64,4,1,64]{3,2,1,0:T(2,128)(2,1)S(1)}, u32[]{:S(2)}, u32[]{:S(2)}) collective-permute-start(bf16[64,4,1,64]{3,2,1,0:T(2,128)(2,1)S(1)} %get-tuple-element.55), channel_id=1, source_target_pairs={{0,1},{2,3},{4,5},{6,7},{8,9},{10,11},{12,13},{14,15},{16,17},{18,... | collective-permute-start | bytes 98312 | tf_op jit(solution)/shard_map/ppermute | solution.py:12
  71.4 46.4 %collective-permute-start.11 = (bf16[64,4,1,64]{3,2,1,0:T(2,128)(2,1)S(1)}, bf16[64,4,1,64]{3,2,1,0:T(2,128)(2,1)S(1)}, u32[]{:S(2)}, u32[]{:S(2)}) collective-permute-start(bf16[64,4,1,64]{3,2,1,0:T(2,128)(2,1)S(1)} %get-tuple-element.56), channel_id=1, source_target_pairs={{1,0},{3,2},{5,4},{7,6},{9,8},{11,10},{13,12},{15,14},{17,16},{19,... | collective-permute-start | bytes 98312 | tf_op jit(solution)/shard_map/ppermute | solution.py:15
  125.9 3.8 %copy-start.4 = (bf16[64,512]{1,0:T(8,128)(2,1)S(1)}, bf16[64,512]{1,0:T(8,128)(2,1)}, u32[]{:S(2)}) copy-start(bf16[64,512]{1,0:T(8,128)(2,1)} %concatenate.232) | copy-start | bytes 196612
  126.9 2.9 %copy-start.9 = (bf16[64,512]{1,0:T(8,128)(2,1)S(1)}, bf16[64,512]{1,0:T(8,128)(2,1)}, u32[]{:S(2)}) copy-start(bf16[64,512]{1,0:T(8,128)(2,1)} %concatenate.236) | copy-start | bytes 196612
  127.2 2.7 %copy-start.7 = (bf16[64,512]{1,0:T(8,128)(2,1)S(1)}, bf16[64,512]{1,0:T(8,128)(2,1)}, u32[]{:S(2)}) copy-start(bf16[64,512]{1,0:T(8,128)(2,1)} %concatenate.239) | copy-start | bytes 196612
  127.7 2.2 %copy-start.5 = (bf16[64,512]{1,0:T(8,128)(2,1)S(1)}, bf16[64,512]{1,0:T(8,128)(2,1)}, u32[]{:S(2)}) copy-start(bf16[64,512]{1,0:T(8,128)(2,1)} %concatenate.244) | copy-start | bytes 196612
  128.0 1.9 copy-start.3
  128.2 1.8 copy-start.8
  128.6 1.5 copy-start.6
  128.8 1.3 copy-start.2
Sparse Core Ops, SparseCore 0:
  62.7 54.2 all-reduce.7
where the time goes:
time: 209 us; the launch traced here: 207 us
  blocking collectives  64.4 us (31%)
  waiting for transfers between devices  58.3 us (28%)
  local copies, waits for them, and re-layouts  31.7 us (15%)
  starting transfers between devices  22.9 us (11%)
  between operations  16.2 us (8%)
  other arithmetic  8.13 us (4%)
  matrix products  5.72 us (3%)
    unnamed x2, waiting for transfers between devices  44.2 us
    psum x1, blocking collectives, shards(): shared = lax.psum((shared[0], shared[1]), 'dp')  19 us
    all_gather x1, blocking collectives, shards(): lax.all_gather(shared[1], ('sx', 'sy'), axis=0, tiled=True)  16.1 us
    concatenate x40, local copies, waits for them, and re-layouts, patches(): stacked = jnp.concatenate(columns, 0)  15.4 us
    ppermute x6, starting transfers between devices, padded_2(): lax.ppermute(lax.slice_in_dim(block, block.shape[dim] - width, None, axis...  15 us
    all_gather x1, blocking collectives, shards(): lax.all_gather(shared[0], ('sx', 'sy'), axis=0, tiled=True)  14.8 us
    unnamed x1, blocking collectives  14.5 us
    ppermute x6, waiting for transfers between devices, padded_2(): lax.ppermute(lax.slice_in_dim(block, 0, width, axis=dim), axis, backward)  14 us
  transfers between devices with their start and end apart: 13, of which 5 were waited for; matrix products, arithmetic and copies ran while one was open for 5% of the time, Pallas kernels for 0%

commit v1 on v0

v1 whole, which is shorter than its diff:
```python
import functools
import math

import jax
import jax.numpy as jnp
from jax import lax
from jax.experimental import pallas as pl
from jax.experimental.pallas import tpu as pltpu
from jax.sharding import PartitionSpec as P

F32 = jnp.float32
BF16 = jnp.bfloat16
NT = (((1,), (1,)), ((), ()))
TN = (((0,), (0,)), ((), ()))


def mm(a, b, dims=(((1,), (0,)), ((), ()))):
    return lax.dot_general(a, b, dims, preferred_element_type=F32)


def one_hot(cond):
    return jnp.where(cond, 1.0, 0.0).astype(BF16)


def local_kernel(
    rim_ref, w1_ref, w2_ref, cot_ref, out_ref, vf, lhs, s_ref, slope_ref, cols, lower,
    *, cin, hx, hy, hz, g_lane, scale_first, scale_second,
):
    nx, ny = hx + 2, hy + 2
    row = ny * hz
    c1 = w1_ref.shape[0]
    win = 16 * cin
    pairs = nx * ny // 2
    lanes = 2 * hz

    vf[...] = rim_ref[...].astype(F32)
    ri = lax.broadcasted_iota(jnp.int32, (2 * lanes, 4 * lanes), 0)
    ci = lax.broadcasted_iota(jnp.int32, (2 * lanes, 4 * lanes), 1)
    sel = one_hot(
        ((ri // lanes) == ((ci % lanes) // hz))
        & ((ri % lanes) == 2 * (ci % hz) + ci // lanes - 1)
    )
    for p in range(pairs):
        for half in range(2):
            cell = 2 * p + half
            cx, cy = cell // ny, cell % ny
            for dx in range(4):
                lhs[
                    p * win + dx * 4 * cin : p * win + (dx + 1) * 4 * cin,
                    half * lanes : (half + 1) * lanes,
                ] = vf[2 * cx + dx, 2 * cin * cy : 2 * cin * cy + 4 * cin, :].astype(BF16)
    picked = mm(lhs[...], sel).astype(BF16)
    for p in range(pairs):
        for o in range(4):
            s_ref[o * win : (o + 1) * win, p * lanes : (p + 1) * lanes] = picked[
                p * win : (p + 1) * win, o * lanes : (o + 1) * lanes
            ]

    wide = w1_ref.shape[1]
    fi = lax.broadcasted_iota(jnp.int32, (4 * win, wide), 0)
    ni = lax.broadcasted_iota(jnp.int32, (4 * win, wide), 1)
    k = ni // cin
    base = (k % 3) * win + (k // 9) * 4 * cin + ((k // 3) % 3) * cin + ni % cin
    diff = fi - base
    folds = [
        one_hot(diff == fz * win + fx * 4 * cin + fy * cin)
        for fx in range(2)
        for fy in range(2)
        for fz in range(2)
    ]
    w1 = w1_ref[...]
    toeplitz = jnp.concatenate([mm(w1, f, NT).astype(BF16) for f in folds], axis=0)

    ix, iy = lax.axis_index("sx"), lax.axis_index("sy")
    last_x, last_y = lax.axis_size("sx") - 1, lax.axis_size("sy") - 1
    lane = lax.broadcasted_iota(jnp.int32, (1, row), 1)
    low_y = jnp.where(iy == 0, hz, 0)
    high_y = jnp.where(iy == last_y, row - hz, row)
    mask_y = jnp.where((lane >= low_y) & (lane < high_y), 1.0, 0.0).astype(F32)
    not_first = jnp.where(lane % hz == 0, 0.0, 1.0).astype(F32)
    not_last = jnp.where(lane % hz == hz - 1, 0.0, 1.0).astype(F32)

    own = hy * hz
    for cx in range(nx):
        here = slice(cx * row, (cx + 1) * row)
        pre = mm(toeplitz, s_ref[:, here])
        t = jnp.exp(-jnp.abs(pre))
        r = 1.0 / (1.0 + t)
        soft = jnp.maximum(pre, 0.0) + jnp.log(1.0 + t)
        sig = jnp.where(pre >= 0, r, t * r)
        hidden = (0.3 * pre + 0.7 * soft).astype(BF16).astype(F32)
        mask = mask_y
        if cx == 0:
            mask = mask * jnp.where(ix == 0, 0.0, 1.0)
        if cx == nx - 1:
            mask = mask * jnp.where(ix == last_x, 0.0, 1.0)
        slope_ref[:, here] = (0.3 + 0.7 * sig) * (mask * 0.125)
        total = hidden[0:c1]
        for s in range(1, 8):
            total = total + hidden[s * c1 : (s + 1) * c1]
        pooled = total * (mask * 0.125)
        three = jnp.concatenate(
            [
                pltpu.roll(pooled, 1, 1) * not_first,
                pooled,
                pltpu.roll(pooled, row - 1, 1) * not_last,
            ],
            axis=0,
        )
        odd = pltpu.roll(three, row - hz, 1).astype(BF16)
        even = three.astype(BF16)
        for a in range(3):
            x = cx - a
            if 0 <= x < hx:
                for b in range(3):
                    at = 3 * c1 * (3 * a + b)
                    piece = odd[:, 0:own] if b == 1 else even[:, b * hz : b * hz + own]
                    cols[at : at + 3 * c1, x * own : (x + 1) * own] = piece

    w2 = w2_ref[...]
    pre2 = mm(w2, cols[...])
    t = jnp.exp(-jnp.abs(pre2))
    r = 1.0 / (1.0 + t)
    slope2 = 0.3 + 0.7 * jnp.where(pre2 >= 0, r, t * r)
    back = (cot_ref[...].astype(F32) * slope2).astype(BF16)
    spread = mm(w2, back, TN)
    second = mm(back, cols[...], NT) * scale_second
    out_ref[...] = jnp.zeros(out_ref.shape, out_ref.dtype)
    out_ref[:, 0 : second.shape[1]] = second.astype(out_ref.dtype)

    for cx in range(nx):
        here = slice(cx * row, (cx + 1) * row)
        blocks = []
        for b in range(3):
            acc = None
            for a in range(3):
                x = cx - a
                if 0 <= x < hx:
                    at = 3 * c1 * (3 * a + b)
                    piece = spread[at : at + 3 * c1, x * own : (x + 1) * own]
                    acc = piece if acc is None else acc + piece
            blocks.append(acc)
        gap = jnp.zeros((3 * c1, 2 * hz), F32)
        grown = (
            jnp.concatenate([blocks[0], gap], axis=1)
            + jnp.concatenate([gap, blocks[2]], axis=1)
            + pltpu.roll(jnp.concatenate([blocks[1], gap], axis=1), hz, 1)
        )
        up = (
            pltpu.roll(grown[0:c1], row - 1, 1) * not_last
            + grown[c1 : 2 * c1]
            + pltpu.roll(grown[2 * c1 : 3 * c1], 1, 1) * not_first
        )
        for s in range(8):
            lower[s * c1 : (s + 1) * c1, here] = (
                up * slope_ref[s * c1 : (s + 1) * c1, here]
            ).astype(BF16)

    products = mm(lower[...], s_ref[...], NT)
    high = products.astype(BF16)
    low = (products - high.astype(F32)).astype(BF16)
    first = jnp.zeros((c1, wide), F32)
    for s in range(8):
        part = slice(s * c1, (s + 1) * c1)
        first = first + mm(high[part], folds[s]) + mm(low[part], folds[s])
    out_ref[0:c1, g_lane : g_lane + wide] = (first * scale_first).astype(out_ref.dtype)


def exchange(block, axis, dim, width):
    count = lax.axis_size(axis)
    size = block.shape[dim]
    top = lax.slice_in_dim(block, size - width, size, axis=dim)
    bottom = lax.slice_in_dim(block, 0, width, axis=dim)
    if count == 2:
        first = lax.axis_index(axis) == 0
        got = lax.ppermute(jnp.where(first, top, bottom), axis, [(0, 1), (1, 0)])
        none = jnp.zeros_like(got)
        low, high = jnp.where(first, none, got), jnp.where(first, got, none)
    else:
        ahead = [(i, i + 1) for i in range(count - 1)]
        low = lax.ppermute(top, axis, ahead)
        high = lax.ppermute(bottom, axis, [(j, i) for i, j in ahead])
    return jnp.concatenate([low, block, high], axis=dim)


def total_over(value, axes):
    for axis in axes:
        count = lax.axis_size(axis)
        if count & (count - 1):
            value = lax.psum(value.astype(F32), axis).astype(value.dtype)
            continue
        step = 1
        while step < count:
            other = lax.ppermute(value, axis, [(i, i ^ step) for i in range(count)])
            value = (value.astype(F32) + other.astype(F32)).astype(value.dtype)
            step *= 2
    return value


def shards(volume, first_weight, second_weight, cotangent):
    samples, cin, wx, wy, wz = volume.shape
    hx, hy, hz = wx // 2, wy // 2, wz // 2
    c1, wide = first_weight.shape
    c2, tall = second_weight.shape
    devices = lax.axis_size("dp") * lax.axis_size("sx") * lax.axis_size("sy")
    coarse = samples * hx * hy * hz * devices
    g_lane = -(-tall // 128) * 128
    width = g_lane + -(-wide // 128) * 128
    nx, ny = hx + 2, hy + 2
    lane = nx * ny * hz
    win = 16 * cin

    block = volume[0].transpose(1, 2, 0, 3)
    rim = exchange(exchange(block, "sy", 1, 3), "sx", 0, 3)
    rim = rim.reshape(wx + 6, (wy + 6) * cin, wz)
    cot = cotangent[0].reshape(c2, hx * hy * hz)

    body = functools.partial(
        local_kernel, cin=cin, hx=hx, hy=hy, hz=hz, g_lane=g_lane,
        scale_first=1.0 / math.sqrt(coarse * 8), scale_second=1.0 / math.sqrt(coarse),
    )
    part = pl.pallas_call(
        body,
        out_shape=jax.ShapeDtypeStruct((c2, width), BF16),
        scratch_shapes=[
            pltpu.VMEM(rim.shape, F32),
            pltpu.VMEM((nx * ny // 2 * win, 2 * wz), BF16),
            pltpu.VMEM((4 * win, lane), BF16),
            pltpu.VMEM((8 * c1, lane), F32),
            pltpu.VMEM((tall, hx * hy * hz), BF16),
            pltpu.VMEM((8 * c1, lane), BF16),
        ],
        name="local_step",
    )(rim, first_weight, second_weight, cot)
    total = total_over(part, ("sx", "sy", "dp")).astype(F32)
    return total[:c1, g_lane : g_lane + wide], total[:, :tall]


def solution(mesh):
    return jax.shard_map(
        shards,
        mesh=mesh,
        in_specs=(P("dp", None, "sx", "sy", None), P(), P(), P("dp", None, "sx", "sy", None)),
        out_specs=(P(), P()),
        check_vma=False,
    )
```

time: 209 us -> 49 us (0.23)
  blocking collectives: 64.4 us -> 0 us
  waiting for transfers between devices: 58.3 us -> 23.1 us
  local copies, waits for them, and re-layouts: 31.7 us -> 2.85 us
  between operations: 16.2 us -> 0.73 us
  starting transfers between devices: 22.9 us -> 14.9 us
  other arithmetic: 8.13 us -> 2.03 us
  matrix products: 5.72 us -> 0 us
  Pallas kernels: 0 us -> 5.07 us
    unnamed x2 -> x0, waiting for transfers between devices: 44.2 us -> none
    all_gather x2 -> x0, blocking collectives: 30.9 us -> none  [the longest x1 16.1 us: shards(): lax.all_gather(shared[1], ('sx', 'sy'), axis=0, tiled=True)]
    psum x1 -> x0, blocking collectives: 19 us -> none  [shards(): shared = lax.psum((shared[0], shared[1]), 'dp')]
    concatenate x41 -> x1, local copies, waits for them, and re-layouts: 15.4 us -> 0.73 us  [exchange(): return jnp.concatenate([low, block, high], axis=dim)]
    unnamed x1 -> x0, blocking collectives: 14.5 us -> none
    ppermute x12 -> x8, waiting for transfers between devices: 14 us -> 23.1 us  [the longest x5 18.1 us: total_over(): other = lax.ppermute(value, axis, [(i, i ^ step) for i in range(count)])]
    ppermute x12 -> x8, starting transfers between devices: 22.9 us -> 14.9 us  [the longest x5 9.13 us: total_over(): other = lax.ppermute(value, axis, [(i, i ^ step) for i in range(count)])]
    dot_general x5 -> x0, matrix products: 5.72 us -> none  [the longest x1 1.62 us: shards(): lax.dot_general(lower, fine_cols, (((1,), (1,)), ((), ())), preferred_ele...]
  transfers between devices with their start and end apart: 13 -> 8, of which waited for: 5 -> 7; matrix products, arithmetic and copies ran while one was open for 5% -> 2% of each run, Pallas kernels for 0% -> 0%
where the time goes in v1:
time: 49 us; the launch traced here: 48.7 us
  waiting for transfers between devices  23.1 us (47%)
  starting transfers between devices  14.9 us (30%)
  Pallas kernels  5.07 us (10%)
  local copies, waits for them, and re-layouts  2.85 us (6%)
  other arithmetic  2.03 us (4%)
  between operations  0.73 us (1%)
    ppermute x5, waiting for transfers between devices, total_over(): other = lax.ppermute(value, axis, [(i, i ^ step) for i in range(count)])  18.1 us
    ppermute x5, starting transfers between devices, total_over(): other = lax.ppermute(value, axis, [(i, i ^ step) for i in range(count)])  9.13 us
    pallas_call x1, Pallas kernels, shards(): pl.pallas_call(body, out_shape=jax.ShapeDtypeStruct((c2, width), BF16), s...  5.07 us
    ppermute x1, waiting for transfers between devices, exchange(): high = lax.ppermute(bottom, axis, [(j, i) for i, j in ahead])  3.32 us
    ppermute x1, starting transfers between devices, exchange(): got = lax.ppermute(jnp.where(first, top, bottom), axis, [(0, 1), (1, 0)])  3.03 us
    ppermute x1, waiting for transfers between devices, exchange(): got = lax.ppermute(jnp.where(first, top, bottom), axis, [(0, 1), (1, 0)])  1.72 us
    ppermute x1, starting transfers between devices, exchange(): low = lax.ppermute(top, axis, ahead)  1.42 us
    slice x2, local copies, waits for them, and re-layouts, shards(): return (total[:c1, g_lane:g_lane + wide], total[:, :tall])  1.31 us
  transfers between devices with their start and end apart: 8, of which 7 were waited for; matrix products, arithmetic and copies ran while one was open for 2% of the time, Pallas kernels for 0%

profile of v1, /device:TPU:0, one launch (start us, length us, event | category | flops | bytes accessed | tf_op | source)
XLA Modules:
  0.0 48.7 jit_solution(15913540680154843349)
XLA Ops:
  0.6 0.9 %slice_select_fusion = bf16[4,3,4,128]{3,1,0,2:T(4,128)(2,1)S(1)} fusion(bf16[4,8,4,128]{3,1,0,2:T(8,128)(2,1)} %bitcast.5, pred[]{:T(512)S(6)} %eq.3), kind=kLoop, calls=%fused_computation.8 | loop fusion | flops 6144 | bytes 36865 | tf_op jit(solution)/shard_map/jit(_where)/select_n | solution.py:176
  1.5 0.0 copy-start
  1.5 3.0 %collective-permute-start = (bf16[4,3,4,128]{3,1,0,2:T(4,128)(2,1)S(1)}, bf16[4,3,4,128]{3,1,0,2:T(4,128)(2,1)S(1)}, u32[]{:S(2)}, u32[]{:S(2)}) collective-permute-start(bf16[4,3,4,128]{3,1,0,2:T(4,128)(2,1)S(1)} %slice_select_fusion), channel_id=1, source_target_pairs={{0,1},{1,0},{2,3},{3,2},{4,5},{5,4},{6,7},{7,6},{8,9},{9,8},{10,11... | collective-permute-start | bytes 36872 | tf_op jit(solution)/shard_map/ppermute | solution.py:176
  4.5 1.7 %collective-permute-done = bf16[4,3,4,128]{3,1,0,2:T(4,128)(2,1)S(1)} collective-permute-done((bf16[4,3,4,128]{3,1,0,2:T(4,128)(2,1)S(1)}, bf16[4,3,4,128]{3,1,0,2:T(4,128)(2,1)S(1)}, u32[]{:S(2)}, u32[]{:S(2)}) %collective-permute-start) | collective-permute-done | bytes 12320 | tf_op jit(solution)/shard_map/ppermute | solution.py:176
  6.3 0.0 copy-done
  6.3 0.0 copy-start.1
  6.4 1.4 %collective-permute-start.1 = (bf16[3,14,4,128]{3,1,0,2:T(8,128)(2,1)S(1)}, bf16[3,14,4,128]{3,1,0,2:T(8,128)(2,1)S(1)}, u32[]{:S(2)}, u32[]{:S(2)}) collective-permute-start(bf16[3,14,4,128]{3,1,0,2:T(8,128)(2,1)S(1)} %get-tuple-element.2), channel_id=1, source_target_pairs={{0,2},{2,4},{4,6},{1,3},{3,5},{5,7},{8,10},{10,12},{12,14},{9,11},... | collective-permute-start | bytes 129032 | tf_op jit(solution)/shard_map/ppermute | solution.py:181
  7.8 1.3 %collective-permute-start.2 = (bf16[3,14,4,128]{3,1,0,2:T(8,128)(2,1)S(1)}, bf16[3,14,4,128]{3,1,0,2:T(8,128)(2,1)S(1)}, u32[]{:S(2)}, u32[]{:S(2)}) collective-permute-start(bf16[3,14,4,128]{3,1,0,2:T(8,128)(2,1)S(1)} %get-tuple-element.3), channel_id=1, source_target_pairs={{2,0},{4,2},{6,4},{3,1},{5,3},{7,5},{10,8},{12,10},{14,12},{11,9},... | collective-permute-start | bytes 129032 | tf_op jit(solution)/shard_map/ppermute | solution.py:182
  9.1 0.0 copy-done.1
  9.1 0.8 %reshape_squeeze.3.cot_ref = bf16[64,512]{1,0:T(8,128)(2,1)} reshape(bf16[1,64,2,4,64]{4,3,2,1,0:T(4,128)(2,1)S(1)} %copy-done.1) | data formatting | bytes 131072 | tf_op jit(solution)/shard_map/reshape;squeeze | solution.py:216
  9.9 0.0 collective-permute-done.1
  9.9 3.3 %collective-permute-done.2 = bf16[3,14,4,128]{3,1,0,2:T(8,128)(2,1)S(1)} collective-permute-done((bf16[3,14,4,128]{3,1,0,2:T(8,128)(2,1)S(1)}, bf16[3,14,4,128]{3,1,0,2:T(8,128)(2,1)S(1)}, u32[]{:S(2)}, u32[]{:S(2)}) %collective-permute-start.2) | collective-permute-done | bytes 43040 | tf_op jit(solution)/shard_map/ppermute | solution.py:182
  13.2 0.1 pad_maximum_fusion
  13.3 0.7 %copy.6 = bf16[10,14,4,128]{3,2,1,0:T(4,128)(2,1)} copy(bf16[10,14,4,128]{3,1,0,2:T(8,128)(2,1)S(1)} %pad_maximum_fusion) | data formatting | bytes 286720 | tf_op jit(solution)/shard_map/concatenate | solution.py:183
  14.0 5.1 %local_step.1 = bf16[64,1024]{1,0:T(8,128)(2,1)} custom-call(bf16[10,56,128]{2,1,0:T(8,128)(2,1)} %bitcast.4, bf16[32,108]{1,0:T(8,128)(2,1)} %w1_ref.1, bf16[64,864]{1,0:T(8,128)(2,1)} %w2_ref.1, bf16[64,512]{1,0:T(8,128)(2,1)} %reshape_squeeze.3.cot_ref), custom_call_target="tpu_custom_call" | custom-call | tf_op jit(solution)/shard_map/local_step/pallas_call | solution.py:222
  19.1 2.8 %collective-permute-start.3 = (bf16[64,1024]{1,0:T(8,128)(2,1)}, bf16[64,1024]{1,0:T(8,128)(2,1)S(1)}, u32[]{:S(2)}, u32[]{:S(2)}) collective-permute-start(bf16[64,1024]{1,0:T(8,128)(2,1)} %local_step.1), channel_id=1, source_target_pairs={{0,2},{2,0},{4,6},{6,4},{1,3},{3,1},{5,7},{7,5},{8,10},{10,8},{12,... | collective-permute-start | bytes 393224 | tf_op jit(solution)/shard_map/ppermute | solution.py:194
  21.8 1.2 %collective-permute-done.3 = bf16[64,1024]{1,0:T(8,128)(2,1)S(1)} collective-permute-done((bf16[64,1024]{1,0:T(8,128)(2,1)}, bf16[64,1024]{1,0:T(8,128)(2,1)S(1)}, u32[]{:S(2)}, u32[]{:S(2)}) %collective-permute-start.3) | collective-permute-done | bytes 131104 | tf_op jit(solution)/shard_map/ppermute | solution.py:194
  23.0 0.9 %add_convert_fusion.4 = bf16[64,1024]{1,0:T(8,128)(2,1)S(1)} fusion(bf16[64,1024]{1,0:T(8,128)(2,1)S(1)} %collective-permute-done.3, bf16[64,1024]{1,0:T(8,128)(2,1)} %local_step.1), kind=kLoop, calls=%fused_computation.4 | loop fusion | flops 262144 | bytes 393216 | tf_op jit(solution)/shard_map/convert_element_type | solution.py:195
  24.0 0.3 collective-permute-start.4
  24.3 5.5 %collective-permute-done.4 = bf16[64,1024]{1,0:T(8,128)(2,1)S(1)} collective-permute-done((bf16[64,1024]{1,0:T(8,128)(2,1)S(1)}, bf16[64,1024]{1,0:T(8,128)(2,1)S(1)}, u32[]{:S(2)}, u32[]{:S(2)}) %collective-permute-start.4) | collective-permute-done | bytes 131104 | tf_op jit(solution)/shard_map/ppermute | solution.py:194
  29.9 1.6 %collective-permute-start.5 = (bf16[64,1024]{1,0:T(8,128)(2,1)S(1)}, bf16[64,1024]{1,0:T(8,128)(2,1)S(1)}, u32[]{:S(2)}, u32[]{:S(2)}) collective-permute-start(bf16[64,1024]{1,0:T(8,128)(2,1)S(1)} %add_convert_fusion.3), channel_id=1, source_target_pairs={{0,1},{1,0},{2,3},{3,2},{4,5},{5,4},{6,7},{7,6},{8,9},{9,8},{10,11... | collective-permute-start | bytes 393224 | tf_op jit(solution)/shard_map/ppermute | solution.py:194
  31.4 3.5 %collective-permute-done.5 = bf16[64,1024]{1,0:T(8,128)(2,1)S(1)} collective-permute-done((bf16[64,1024]{1,0:T(8,128)(2,1)S(1)}, bf16[64,1024]{1,0:T(8,128)(2,1)S(1)}, u32[]{:S(2)}, u32[]{:S(2)}) %collective-permute-start.5) | collective-permute-done | bytes 131104 | tf_op jit(solution)/shard_map/ppermute | solution.py:194
  34.9 1.6 %collective-permute-start.6 = (bf16[64,1024]{1,0:T(8,128)(2,1)S(1)}, bf16[64,1024]{1,0:T(8,128)(2,1)S(1)}, u32[]{:S(2)}, u32[]{:S(2)}) collective-permute-start(bf16[64,1024]{1,0:T(8,128)(2,1)S(1)} %add_convert_fusion.2), channel_id=1, source_target_pairs={{0,8},{8,0},{16,24},{24,16},{1,9},{9,1},{17,25},{25,17},{2,10},{10... | collective-permute-start | bytes 393224 | tf_op jit(solution)/shard_map/ppermute | solution.py:194
  36.6 3.4 %collective-permute-done.6 = bf16[64,1024]{1,0:T(8,128)(2,1)S(1)} collective-permute-done((bf16[64,1024]{1,0:T(8,128)(2,1)S(1)}, bf16[64,1024]{1,0:T(8,128)(2,1)S(1)}, u32[]{:S(2)}, u32[]{:S(2)}) %collective-permute-start.6) | collective-permute-done | bytes 131104 | tf_op jit(solution)/shard_map/ppermute | solution.py:194
  40.0 2.9 %collective-permute-start.7 = (bf16[64,1024]{1,0:T(8,128)(2,1)S(1)}, bf16[64,1024]{1,0:T(8,128)(2,1)S(1)}, u32[]{:S(2)}, u32[]{:S(2)}) collective-permute-start(bf16[64,1024]{1,0:T(8,128)(2,1)S(1)} %add_convert_fusion.1), channel_id=1, source_target_pairs={{0,16},{8,24},{16,0},{24,8},{1,17},{9,25},{17,1},{25,9},{2,18},{10... | collective-permute-start | bytes 393224 | tf_op jit(solution)/shard_map/ppermute | solution.py:194
  42.9 4.5 %collective-permute-done.7 = bf16[64,1024]{1,0:T(8,128)(2,1)S(1)} collective-permute-done((bf16[64,1024]{1,0:T(8,128)(2,1)S(1)}, bf16[64,1024]{1,0:T(8,128)(2,1)S(1)}, u32[]{:S(2)}, u32[]{:S(2)}) %collective-permute-start.7) | collective-permute-done | bytes 131104 | tf_op jit(solution)/shard_map/ppermute | solution.py:194
  47.4 0.6 %slice.28 = f32[32,108]{1,0:T(8,128)} slice(f32[64,1024]{1,0:T(8,128)S(1)} %fusion), slice={[0:32], [896:1004]} | slice | bytes 27648 | tf_op jit(solution)/shard_map/slice | solution.py:236
  48.0 0.7 %slice.29 = f32[64,864]{1,0:T(8,128)} slice(f32[64,1024]{1,0:T(8,128)S(1)} %fusion), slice={[0:64], [0:864]} | slice | bytes 442368 | tf_op jit(solution)/shard_map/slice | solution.py:236
  (7 shorter events, 0.2 us)
Async XLA Ops:
  1.5 4.8 %copy-start = (bf16[1,4,4,8,128]{4,3,2,1,0:T(8,128)(2,1)S(1)}, bf16[1,4,4,8,128]{4,3,2,1,0:T(8,128)(2,1)}, u32[]{:S(2)}) copy-start(bf16[1,4,4,8,128]{4,3,2,1,0:T(8,128)(2,1)} %param.4) | copy-start | bytes 98308
  1.5 4.8 %collective-permute-start = (bf16[4,3,4,128]{3,1,0,2:T(4,128)(2,1)S(1)}, bf16[4,3,4,128]{3,1,0,2:T(4,128)(2,1)S(1)}, u32[]{:S(2)}, u32[]{:S(2)}) collective-permute-start(bf16[4,3,4,128]{3,1,0,2:T(4,128)(2,1)S(1)} %slice_select_fusion), channel_id=1, source_target_pairs={{0,1},{1,0},{2,3},{3,2},{4,5},{5,4},{6,7},{7,6},{8,9},{9,8},{10,11... | collective-permute-start | bytes 36872 | tf_op jit(solution)/shard_map/ppermute | solution.py:176
  6.3 2.8 %copy-start.1 = (bf16[1,64,2,4,64]{4,3,2,1,0:T(4,128)(2,1)S(1)}, bf16[1,64,2,4,64]{4,3,2,1,0:T(4,128)(2,1)}, u32[]{:S(2)}) copy-start(bf16[1,64,2,4,64]{4,3,2,1,0:T(4,128)(2,1)} %param.7) | copy-start | bytes 196612
  6.4 3.5 %collective-permute-start.1 = (bf16[3,14,4,128]{3,1,0,2:T(8,128)(2,1)S(1)}, bf16[3,14,4,128]{3,1,0,2:T(8,128)(2,1)S(1)}, u32[]{:S(2)}, u32[]{:S(2)}) collective-permute-start(bf16[3,14,4,128]{3,1,0,2:T(8,128)(2,1)S(1)} %get-tuple-element.2), channel_id=1, source_target_pairs={{0,2},{2,4},{4,6},{1,3},{3,5},{5,7},{8,10},{10,12},{12,14},{9,11},... | collective-permute-start | bytes 129032 | tf_op jit(solution)/shard_map/ppermute | solution.py:181
  7.8 5.4 %collective-permute-start.2 = (bf16[3,14,4,128]{3,1,0,2:T(8,128)(2,1)S(1)}, bf16[3,14,4,128]{3,1,0,2:T(8,128)(2,1)S(1)}, u32[]{:S(2)}, u32[]{:S(2)}) collective-permute-start(bf16[3,14,4,128]{3,1,0,2:T(8,128)(2,1)S(1)} %get-tuple-element.3), channel_id=1, source_target_pairs={{2,0},{4,2},{6,4},{3,1},{5,3},{7,5},{10,8},{12,10},{14,12},{11,9},... | collective-permute-start | bytes 129032 | tf_op jit(solution)/shard_map/ppermute | solution.py:182
  19.1 4.0 %collective-permute-start.3 = (bf16[64,1024]{1,0:T(8,128)(2,1)}, bf16[64,1024]{1,0:T(8,128)(2,1)S(1)}, u32[]{:S(2)}, u32[]{:S(2)}) collective-permute-start(bf16[64,1024]{1,0:T(8,128)(2,1)} %local_step.1), channel_id=1, source_target_pairs={{0,2},{2,0},{4,6},{6,4},{1,3},{3,1},{5,7},{7,5},{8,10},{10,8},{12,... | collective-permute-start | bytes 393224 | tf_op jit(solution)/shard_map/ppermute | solution.py:194
  24.0 5.8 %collective-permute-start.4 = (bf16[64,1024]{1,0:T(8,128)(2,1)S(1)}, bf16[64,1024]{1,0:T(8,128)(2,1)S(1)}, u32[]{:S(2)}, u32[]{:S(2)}) collective-permute-start(bf16[64,1024]{1,0:T(8,128)(2,1)S(1)} %add_convert_fusion.4), channel_id=1, source_target_pairs={{0,4},{2,6},{4,0},{6,2},{1,5},{3,7},{5,1},{7,3},{8,12},{10,14},{12... | collective-permute-start | bytes 393224 | tf_op jit(solution)/shard_map/ppermute | solution.py:194
  29.9 5.0 %collective-permute-start.5 = (bf16[64,1024]{1,0:T(8,128)(2,1)S(1)}, bf16[64,1024]{1,0:T(8,128)(2,1)S(1)}, u32[]{:S(2)}, u32[]{:S(2)}) collective-permute-start(bf16[64,1024]{1,0:T(8,128)(2,1)S(1)} %add_convert_fusion.3), channel_id=1, source_target_pairs={{0,1},{1,0},{2,3},{3,2},{4,5},{5,4},{6,7},{7,6},{8,9},{9,8},{10,11... | collective-permute-start | bytes 393224 | tf_op jit(solution)/shard_map/ppermute | solution.py:194
  34.9 5.0 %collective-permute-start.6 = (bf16[64,1024]{1,0:T(8,128)(2,1)S(1)}, bf16[64,1024]{1,0:T(8,128)(2,1)S(1)}, u32[]{:S(2)}, u32[]{:S(2)}) collective-permute-start(bf16[64,1024]{1,0:T(8,128)(2,1)S(1)} %add_convert_fusion.2), channel_id=1, source_target_pairs={{0,8},{8,0},{16,24},{24,16},{1,9},{9,1},{17,25},{25,17},{2,10},{10... | collective-permute-start | bytes 393224 | tf_op jit(solution)/shard_map/ppermute | solution.py:194
  40.0 7.3 %collective-permute-start.7 = (bf16[64,1024]{1,0:T(8,128)(2,1)S(1)}, bf16[64,1024]{1,0:T(8,128)(2,1)S(1)}, u32[]{:S(2)}, u32[]{:S(2)}) collective-permute-start(bf16[64,1024]{1,0:T(8,128)(2,1)S(1)} %add_convert_fusion.1), channel_id=1, source_target_pairs={{0,16},{8,24},{16,0},{24,8},{1,17},{9,25},{17,1},{25,9},{2,18},{10... | collective-permute-start | bytes 393224 | tf_op jit(solution)/shard_map/ppermute | solution.py:194

commit v2 on v1

--- a/solution.py
+++ b/solution.py
@@ -11,6 +11,7 @@
 F32 = jnp.float32
 BF16 = jnp.bfloat16
 NT = (((1,), (1,)), ((), ()))
+RIM = 3
 TN = (((0,), (0,)), ((), ()))
 
 
@@ -23,7 +24,8 @@
 
 
 def local_kernel(
-    rim_ref, w1_ref, w2_ref, cot_ref, out_ref, vf, lhs, s_ref, slope_ref, cols, lower,
+    block_ref, near_ref, far_ref, side_ref, diag_ref, w1_ref, w2_ref, cot_ref, keep_ref, send_ref,
+    vf, lhs, s_ref, slope_ref, cols, lower,
     *, cin, hx, hy, hz, g_lane, scale_first, scale_second,
 ):
     nx, ny = hx + 2, hy + 2
@@ -33,7 +35,24 @@
     pairs = nx * ny // 2
     lanes = 2 * hz
 
-    vf[...] = rim_ref[...].astype(F32)
+    ix, iy = lax.axis_index("sx"), lax.axis_index("sy")
+    last_x, last_y = lax.axis_size("sx") - 1, lax.axis_size("sy") - 1
+    odd_x = ix % 2
+    wx, rows = 2 * hx, 2 * hy * cin
+    lip = RIM * cin
+    near_at = jnp.where(odd_x == 1, 0, RIM + wx)
+    far_at = RIM + wx - near_at
+    vf[RIM : RIM + wx, lip : lip + rows, :] = block_ref[...].astype(F32)
+    vf[pl.ds(near_at, RIM), lip : lip + rows, :] = near_ref[...].astype(F32)
+    vf[pl.ds(far_at, RIM), lip : lip + rows, :] = far_ref[...].astype(F32)
+    for at, count, piece in (
+        (RIM, wx, side_ref[0:wx]),
+        (near_at, RIM, side_ref[wx : wx + RIM]),
+        (far_at, RIM, diag_ref[...]),
+    ):
+        piece = piece.astype(F32)
+        vf[pl.ds(at, count), 0:lip, :] = jnp.where(iy == 0, 0.0, piece)
+        vf[pl.ds(at, count), lip + rows : 2 * lip + rows, :] = jnp.where(iy == 0, piece, 0.0)
     ri = lax.broadcasted_iota(jnp.int32, (2 * lanes, 4 * lanes), 0)
     ci = lax.broadcasted_iota(jnp.int32, (2 * lanes, 4 * lanes), 1)
     sel = one_hot(
@@ -71,8 +90,6 @@
     w1 = w1_ref[...]
     toeplitz = jnp.concatenate([mm(w1, f, NT).astype(BF16) for f in folds], axis=0)
 
-    ix, iy = lax.axis_index("sx"), lax.axis_index("sy")
-    last_x, last_y = lax.axis_size("sx") - 1, lax.axis_size("sy") - 1
     lane = lax.broadcasted_iota(jnp.int32, (1, row), 1)
     low_y = jnp.where(iy == 0, hz, 0)
     high_y = jnp.where(iy == last_y, row - hz, row)
@@ -125,8 +142,13 @@
     back = (cot_ref[...].astype(F32) * slope2).astype(BF16)
     spread = mm(w2, back, TN)
     second = mm(back, cols[...], NT) * scale_second
-    out_ref[...] = jnp.zeros(out_ref.shape, out_ref.dtype)
-    out_ref[:, 0 : second.shape[1]] = second.astype(out_ref.dtype)
+    tall = second.shape[1]
+    half = second.shape[0] // 2
+    is_odd = odd_x == 1
+    keep_ref[...] = jnp.zeros(keep_ref.shape, keep_ref.dtype)
+    send_ref[...] = jnp.zeros(send_ref.shape, send_ref.dtype)
+    keep_ref[:, 0:tall] = jnp.where(is_odd, second[half:], second[:half])
+    send_ref[:, 0:tall] = jnp.where(is_odd, second[:half], second[half:]).astype(BF16)
 
     for cx in range(nx):
         here = slice(cx * row, (cx + 1) * row)
@@ -163,38 +185,42 @@
     for s in range(8):
         part = slice(s * c1, (s + 1) * c1)
         first = first + mm(high[part], folds[s]) + mm(low[part], folds[s])
-    out_ref[0:c1, g_lane : g_lane + wide] = (first * scale_first).astype(out_ref.dtype)
-
-
-def exchange(block, axis, dim, width):
-    count = lax.axis_size(axis)
-    size = block.shape[dim]
-    top = lax.slice_in_dim(block, size - width, size, axis=dim)
-    bottom = lax.slice_in_dim(block, 0, width, axis=dim)
-    if count == 2:
-        first = lax.axis_index(axis) == 0
-        got = lax.ppermute(jnp.where(first, top, bottom), axis, [(0, 1), (1, 0)])
-        none = jnp.zeros_like(got)
-        low, high = jnp.where(first, none, got), jnp.where(first, got, none)
-    else:
-        ahead = [(i, i + 1) for i in range(count - 1)]
-        low = lax.ppermute(top, axis, ahead)
-        high = lax.ppermute(bottom, axis, [(j, i) for i, j in ahead])
-    return jnp.concatenate([low, block, high], axis=dim)
-
-
-def total_over(value, axes):
-    for axis in axes:
-        count = lax.axis_size(axis)
-        if count & (count - 1):
-            value = lax.psum(value.astype(F32), axis).astype(value.dtype)
+    first = first * scale_first
+    keep_ref[0:c1, g_lane : g_lane + wide] = jnp.where(is_odd, 0.0, first)
+    send_ref[0:c1, g_lane : g_lane + wide] = jnp.where(is_odd, first, 0.0).astype(BF16)
+
+
+def join_kernel(mine_ref, other_ref, first_ref, second_ref, *, g_lane):
+    is_odd = lax.axis_index("sx") % 2 == 1
+    mine, other = mine_ref[...].astype(F32), other_ref[...].astype(F32)
+    upper = jnp.where(is_odd, other, mine)
+    half = mine.shape[0]
+    tall = second_ref.shape[1]
+    c1, wide = first_ref.shape
+    second_ref[0:half, :] = upper[:, 0:tall]
+    second_ref[half:, :] = jnp.where(is_odd, mine, other)[:, 0:tall]
+    first_ref[...] = upper[0:c1, g_lane : g_lane + wide]
+
+
+def swap(value, axes, mask):
+    count = lax.axis_size(axes)
+    return lax.ppermute(value, axes, [(i, i ^ mask) for i in range(count)])
+
+
+def total_over(value, axes, masks):
+    for at in range(0, len(masks), 2):
+        pair = masks[at : at + 2]
+        if len(pair) == 1:
+            value = (value.astype(F32) + swap(value, axes, pair[0]).astype(F32)).astype(BF16)
             continue
-        step = 1
-        while step < count:
-            other = lax.ppermute(value, axis, [(i, i ^ step) for i in range(count)])
-            value = (value.astype(F32) + other.astype(F32)).astype(value.dtype)
-            step *= 2
+        m, n = pair
+        one, two, three = (swap(value, axes, x).astype(F32) for x in (m, n, m ^ n))
+        value = ((value.astype(F32) + one) + (two + three)).astype(BF16)
     return value
+
+
+def bits(count):
+    return [1 << i for i in range(count.bit_length() - 1)]
 
 
 def shards(volume, first_weight, second_weight, cotangent):
@@ -210,20 +236,39 @@
     lane = nx * ny * hz
     win = 16 * cin
 
-    block = volume[0].transpose(1, 2, 0, 3)
-    rim = exchange(exchange(block, "sy", 1, 3), "sx", 0, 3)
-    rim = rim.reshape(wx + 6, (wy + 6) * cin, wz)
+    count_x, count_y = lax.axis_size("sx"), lax.axis_size("sy")
+    assert count_y == 2 and count_x & (count_x - 1) == 0 and 2 * c1 == c2
+    odd_x = lax.axis_index("sx") % 2 == 1
+    low_y = lax.axis_index("sy") == 0
+    lip = RIM * cin
+    block = volume[0].transpose(1, 2, 0, 3).reshape(wx, wy * cin, wz)
+
+    def rim_y(piece):
+        return jnp.where(low_y, piece[:, -lip:], piece[:, :lip])
+
+    inner = jnp.where(odd_x, block[:RIM], block[-RIM:])
+    outer = jnp.where(odd_x, block[-RIM:], block[:RIM])
+    near = swap(inner, "sx", 1)
+    pairs = [(i, i + 1) for i in range(1, count_x - 1, 2)]
+    pairs = pairs + [(j, i) for i, j in pairs]
+    far = lax.ppermute(outer, "sx", pairs)
+    crossed = [(2 * i + t, 2 * j + 1 - t) for i, j in pairs for t in range(2)]
+    diag = lax.ppermute(rim_y(outer), ("sx", "sy"), crossed)
+    side = swap(jnp.concatenate([rim_y(block), rim_y(near)], axis=0), "sy", 1)
     cot = cotangent[0].reshape(c2, hx * hy * hz)
 
     body = functools.partial(
         local_kernel, cin=cin, hx=hx, hy=hy, hz=hz, g_lane=g_lane,
         scale_first=1.0 / math.sqrt(coarse * 8), scale_second=1.0 / math.sqrt(coarse),
     )
-    part = pl.pallas_call(
+    keep, send = pl.pallas_call(
         body,
-        out_shape=jax.ShapeDtypeStruct((c2, width), BF16),
+        out_shape=(
+            jax.ShapeDtypeStruct((c2 // 2, width), F32),
+            jax.ShapeDtypeStruct((c2 // 2, width), BF16),
+        ),
         scratch_shapes=[
-            pltpu.VMEM(rim.shape, F32),
+            pltpu.VMEM((wx + 2 * RIM, (wy + 2 * RIM) * cin, wz), F32),
             pltpu.VMEM((nx * ny // 2 * win, 2 * wz), BF16),
             pltpu.VMEM((4 * win, lane), BF16),
             pltpu.VMEM((8 * c1, lane), F32),
@@ -231,9 +276,18 @@
             pltpu.VMEM((8 * c1, lane), BF16),
         ],
         name="local_step",
-    )(rim, first_weight, second_weight, cot)
-    total = total_over(part, ("sx", "sy", "dp")).astype(F32)
-    return total[:c1, g_lane : g_lane + wide], total[:, :tall]
+    )(block, near, far, side, diag, first_weight, second_weight, cot)
+    mine = (keep + swap(send, "sx", 1).astype(F32)).astype(BF16)
+    mine = total_over(mine, ("sx", "sy"), [1] + [2 * m for m in bits(count_x)[1:]])
+    mine = total_over(mine, ("dp",), bits(lax.axis_size("dp")))
+    return pl.pallas_call(
+        functools.partial(join_kernel, g_lane=g_lane),
+        out_shape=(
+            jax.ShapeDtypeStruct((c1, wide), F32),
+            jax.ShapeDtypeStruct((c2, tall), F32),
+        ),
+        name="join",
+    )(mine, swap(mine, "sx", 1))
 
 
 def solution(mesh):

time: 49 us -> 42.5 us (0.87)
  waiting for transfers between devices: 23.1 us -> 10.3 us
  starting transfers between devices: 14.9 us -> 19.7 us
  Pallas kernels: 5.07 us -> 6.73 us
  other arithmetic: 2.03 us -> 1.04 us
  local copies, waits for them, and re-layouts: 2.85 us -> 3.61 us
    ppermute x8 -> x12, waiting for transfers between devices: 23.1 us -> 10.3 us  [the longest x10 10.3 us: swap(): return lax.ppermute(value, axes, [(i, i ^ mask) for i in range(count)])]
    ppermute x8 -> x12, starting transfers between devices: 14.9 us -> 19.7 us  [the longest x10 18.2 us: swap(): return lax.ppermute(value, axes, [(i, i ^ mask) for i in range(count)])]
    unnamed x4 -> x18, local copies, waits for them, and re-layouts: 0.01 us -> 2.8 us
    pallas_call x1 -> x2, Pallas kernels: 5.07 us -> 6.73 us  [the longest x1 5.14 us: shards(): pl.pallas_call(body, out_shape=(jax.ShapeDtypeStruct((c2 // 2, width), F3...]
    slice x3 -> x0, local copies, waits for them, and re-layouts: 1.33 us -> none  [the longest x2 1.31 us: shards(): return (total[:c1, g_lane:g_lane + wide], total[:, :tall])]
    select_n x2 -> x4, other arithmetic: 0.87 us -> 0.03 us  [the longest x3 0.03 us: rim_y(): return jnp.where(low_y, piece[:, -lip:], piece[:, :lip])]
    concatenate x1 -> x0, local copies, waits for them, and re-layouts: 0.73 us -> none  [exchange(): return jnp.concatenate([low, block, high], axis=dim)]
    convert_element_type x5 -> x3, other arithmetic: 1.07 us -> 1 us  [the longest x1 0.92 us: shards(): mine = (keep + swap(send, 'sx', 1).astype(F32)).astype(BF16)]
  transfers between devices with their start and end apart: 8 -> 12, of which waited for: 7 -> 8; matrix products, arithmetic and copies ran while one was open for 2% -> 2% of each run, Pallas kernels for 0% -> 0%
where the time goes in v2:
time: 42.5 us; the launch traced here: 42.2 us
  starting transfers between devices  19.7 us (46%)
  waiting for transfers between devices  10.3 us (24%)
  Pallas kernels  6.73 us (16%)
  local copies, waits for them, and re-layouts  3.61 us (8%)
  other arithmetic  1.04 us (2%)
  between operations  0.81 us (2%)
    ppermute x10, starting transfers between devices, swap(): return lax.ppermute(value, axes, [(i, i ^ mask) for i in range(count)])  18.2 us
    ppermute x10, waiting for transfers between devices, swap(): return lax.ppermute(value, axes, [(i, i ^ mask) for i in range(count)])  10.3 us
    pallas_call x1, Pallas kernels, shards(): pl.pallas_call(body, out_shape=(jax.ShapeDtypeStruct((c2 // 2, width), F3...  5.14 us
    unnamed x18, local copies, waits for them, and re-layouts  2.8 us
    pallas_call x1, Pallas kernels, shards(): pl.pallas_call(functools.partial(join_kernel, g_lane=g_lane), out_shape=(...  1.58 us
    convert_element_type x1, other arithmetic, shards(): mine = (keep + swap(send, 'sx', 1).astype(F32)).astype(BF16)  0.92 us
  transfers between devices with their start and end apart: 12, of which 8 were waited for; matrix products, arithmetic and copies ran while one was open for 2% of the time, Pallas kernels for 0%

profile of v2, /device:TPU:0, one launch (start us, length us, event | category | flops | bytes accessed | tf_op | source)
XLA Modules:
  0.0 42.2 jit_solution(12408501884939737064)
XLA Ops:
  0.6 0.0 copy-start.2
  0.7 0.7 %copy-done.2 = bf16[1,4,4,8,128]{4,3,2,1,0:T(8,128)(2,1)S(1)} copy-done((bf16[1,4,4,8,128]{4,3,2,1,0:T(8,128)(2,1)S(1)}, bf16[1,4,4,8,128]{4,3,2,1,0:T(8,128)(2,1)}, u32[]{:S(2)}) %copy-start.2) | copy-done | bytes 32792
  1.4 0.6 %collective-permute-start = (bf16[3,32,128]{2,1,0:T(8,128)(2,1)S(1)}, bf16[3,32,128]{2,1,0:T(8,128)(2,1)S(1)}, u32[]{:S(2)}, u32[]{:S(2)}) collective-permute-start(bf16[3,32,128]{2,1,0:T(8,128)(2,1)S(1)} %bitcast.12), channel_id=1, source_target_pairs={{0,2},{2,0},{4,6},{6,4},{1,3},{3,1},{5,7},{7,5},{8,10},{10,8},{12,... | collective-permute-start | bytes 73736 | tf_op jit(solution)/shard_map/ppermute | solution.py:207
  2.0 0.0 copy-start.3
  2.0 0.8 %collective-permute-start.1 = (bf16[3,32,128]{2,1,0:T(8,128)(2,1)S(1)}, bf16[3,32,128]{2,1,0:T(8,128)(2,1)S(1)}, u32[]{:S(2)}, u32[]{:S(2)}) collective-permute-start(bf16[3,32,128]{2,1,0:T(8,128)(2,1)S(1)} %bitcast.10), channel_id=1, source_target_pairs={{2,4},{4,2},{3,5},{5,3},{10,12},{12,10},{11,13},{13,11},{18,20},{2... | collective-permute-start | bytes 73736 | tf_op jit(solution)/shard_map/ppermute | solution.py:254
  2.8 0.0 copy-start
  2.9 0.0 collective-permute-done.near_ref
  2.9 0.0 copy-start.4
  2.9 0.5 %copy-done = bf16[4,8,4,128]{3,2,1,0:T(4,128)(2,1)} copy-done((bf16[4,8,4,128]{3,2,1,0:T(4,128)(2,1)}, bf16[4,8,4,128]{3,2,1,0:T(4,128)(2,1)S(1)}, u32[]{:S(2)}) %copy-start) | copy-done | bytes 32792
  3.4 0.0 copy-done.4
  3.5 2.8 %collective-permute-start.2 = (bf16[7,12,128]{2,1,0:T(8,128)(2,1)S(1)}, bf16[7,12,128]{2,1,0:T(8,128)(2,1)S(1)}, u32[]{:S(2)}, u32[]{:S(2)}) collective-permute-start(bf16[7,12,128]{2,1,0:T(8,128)(2,1)S(1)} %pad_maximum_fusion), channel_id=1, source_target_pairs={{0,1},{1,0},{2,3},{3,2},{4,5},{5,4},{6,7},{7,6},{8,9},{9,8},{10,11... | collective-permute-start | bytes 64520 | tf_op jit(solution)/shard_map/ppermute | solution.py:207
  6.3 0.7 %collective-permute-start.3 = (bf16[3,12,128]{2,1,0:T(8,128)(2,1)S(1)}, bf16[3,12,128]{2,1,0:T(8,128)(2,1)S(1)}, u32[]{:S(2)}, u32[]{:S(2)}) collective-permute-start(bf16[3,12,128]{2,1,0:T(8,128)(2,1)S(1)} %slice_select_fusion.1), channel_id=1, source_target_pairs={{2,5},{3,4},{4,3},{5,2},{10,13},{11,12},{12,11},{13,10},{18,21},{1... | collective-permute-start | bytes 27656 | tf_op jit(solution)/shard_map/ppermute | solution.py:256
  6.9 0.0 copy-done.3
  7.0 0.8 %reshape_squeeze.3.cot_ref = bf16[64,512]{1,0:T(8,128)(2,1)} reshape(bf16[1,64,2,4,64]{4,3,2,1,0:T(4,128)(2,1)S(1)} %copy-done.3) | data formatting | bytes 131072 | tf_op jit(solution)/shard_map/reshape;squeeze | solution.py:258
  7.7 0.0 collective-permute-done.3.diag_ref
  7.7 0.0 copy-start.8
  7.7 0.0 collective-permute-done.1.far_ref
  7.7 0.0 copy-start.7
  7.7 0.4 collective-permute-done.2.side_ref
  8.1 0.2 copy-done.8
  8.3 0.0 copy-done.7
  8.3 0.0 copy-start.6
  8.3 0.6 %copy-done.6 = bf16[7,12,128]{2,1,0:T(8,128)(2,1)} copy-done((bf16[7,12,128]{2,1,0:T(8,128)(2,1)}, bf16[7,12,128]{2,1,0:T(8,128)(2,1)S(1)}, u32[]{:S(2)}) %copy-start.6) | copy-done | bytes 21528
  8.9 5.1 %local_step.1 = (f32[32,1024]{1,0:T(8,128)}, bf16[32,1024]{1,0:T(8,128)(2,1)}) custom-call(bf16[4,32,128]{2,1,0:T(8,128)(2,1)} %bitcast.7, bf16[3,32,128]{2,1,0:T(8,128)(2,1)} %copy-done.4, bf16[3,32,128]{2,1,0:T(8,128)(2,1)} %copy-done.7, bf16[7,12,128]{2,1,0:T(8,128)(2,1)} %copy-done.6, bf16[3,12,128]{2,1,0:T(8,128)(2,1)} %copy-done.8, ...), custom_call_target="tpu_custom_call" | custom-call | tf_op jit(solution)/shard_map/local_step/pallas_call | solution.py:264
  14.1 6.8 %collective-permute-start.4 = (bf16[32,1024]{1,0:T(8,128)(2,1)}, bf16[32,1024]{1,0:T(8,128)(2,1)S(1)}, u32[]{:S(2)}, u32[]{:S(2)}) collective-permute-start(bf16[32,1024]{1,0:T(8,128)(2,1)} %get-tuple-element.5), channel_id=1, source_target_pairs={{0,2},{2,0},{4,6},{6,4},{1,3},{3,1},{5,7},{7,5},{8,10},{10,8},{12,... | collective-permute-start | bytes 196616 | tf_op jit(solution)/shard_map/ppermute | solution.py:207
  20.9 1.1 %collective-permute-done.4 = bf16[32,1024]{1,0:T(8,128)(2,1)S(1)} collective-permute-done((bf16[32,1024]{1,0:T(8,128)(2,1)}, bf16[32,1024]{1,0:T(8,128)(2,1)S(1)}, u32[]{:S(2)}, u32[]{:S(2)}) %collective-permute-start.4) | collective-permute-done | bytes 65568 | tf_op jit(solution)/shard_map/ppermute | solution.py:207
  22.0 0.9 %add_convert_fusion.2 = bf16[32,1024]{1,0:T(8,128)(2,1)S(1)} fusion(f32[32,1024]{1,0:T(8,128)} %get-tuple-element.4, bf16[32,1024]{1,0:T(8,128)(2,1)S(1)} %collective-permute-done.4), kind=kLoop, calls=%fused_computation.2 | loop fusion | flops 98304 | bytes 262144 | tf_op jit(solution)/shard_map/convert_element_type | solution.py:280
  22.9 0.6 %collective-permute-start.7 = (bf16[32,1024]{1,0:T(8,128)(2,1)S(1)}, bf16[32,1024]{1,0:T(8,128)(2,1)S(1)}, u32[]{:S(2)}, u32[]{:S(2)}) collective-permute-start(bf16[32,1024]{1,0:T(8,128)(2,1)S(1)} %add_convert_fusion.2), channel_id=1, source_target_pairs={{0,5},{1,4},{2,7},{3,6},{4,1},{5,0},{6,3},{7,2},{8,13},{9,12},{10,... | collective-permute-start | bytes 196616 | tf_op jit(solution)/shard_map/ppermute | solution.py:207
  23.6 1.4 %collective-permute-start.6 = (bf16[32,1024]{1,0:T(8,128)(2,1)S(1)}, bf16[32,1024]{1,0:T(8,128)(2,1)S(1)}, u32[]{:S(2)}, u32[]{:S(2)}) collective-permute-start(bf16[32,1024]{1,0:T(8,128)(2,1)S(1)} %add_convert_fusion.2), channel_id=1, source_target_pairs={{0,4},{1,5},{2,6},{3,7},{4,0},{5,1},{6,2},{7,3},{8,12},{9,13},{10,... | collective-permute-start | bytes 196616 | tf_op jit(solution)/shard_map/ppermute | solution.py:207
  25.0 1.5 %collective-permute-start.5 = (bf16[32,1024]{1,0:T(8,128)(2,1)S(1)}, bf16[32,1024]{1,0:T(8,128)(2,1)S(1)}, u32[]{:S(2)}, u32[]{:S(2)}) collective-permute-start(bf16[32,1024]{1,0:T(8,128)(2,1)S(1)} %add_convert_fusion.2), channel_id=1, source_target_pairs={{0,1},{1,0},{2,3},{3,2},{4,5},{5,4},{6,7},{7,6},{8,9},{9,8},{10,11... | collective-permute-start | bytes 196616 | tf_op jit(solution)/shard_map/ppermute | solution.py:207
  26.5 2.4 %collective-permute-done.7 = bf16[32,1024]{1,0:T(8,128)(2,1)S(1)} collective-permute-done((bf16[32,1024]{1,0:T(8,128)(2,1)S(1)}, bf16[32,1024]{1,0:T(8,128)(2,1)S(1)}, u32[]{:S(2)}, u32[]{:S(2)}) %collective-permute-start.7) | collective-permute-done | bytes 65568 | tf_op jit(solution)/shard_map/ppermute | solution.py:207
  28.9 0.1 collective-permute-done.6
  29.0 0.3 collective-permute-done.5
  29.3 3.8 %collective-permute-start.10 = (bf16[32,1024]{1,0:T(8,128)(2,1)S(1)}, bf16[32,1024]{1,0:T(8,128)(2,1)S(1)}, u32[]{:S(2)}, u32[]{:S(2)}) collective-permute-start(bf16[32,1024]{1,0:T(8,128)(2,1)S(1)} %add_convert_fusion.1), channel_id=1, source_target_pairs={{0,24},{8,16},{16,8},{24,0},{1,25},{9,17},{17,9},{25,1},{2,26},{10... | collective-permute-start | bytes 196616 | tf_op jit(solution)/shard_map/ppermute | solution.py:207
  33.1 0.0 collective-permute-start.9
  33.1 0.7 %collective-permute-start.8 = (bf16[32,1024]{1,0:T(8,128)(2,1)S(1)}, bf16[32,1024]{1,0:T(8,128)(2,1)S(1)}, u32[]{:S(2)}, u32[]{:S(2)}) collective-permute-start(bf16[32,1024]{1,0:T(8,128)(2,1)S(1)} %add_convert_fusion.1), channel_id=1, source_target_pairs={{0,8},{8,0},{16,24},{24,16},{1,9},{9,1},{17,25},{25,17},{2,10},{10... | collective-permute-start | bytes 196616 | tf_op jit(solution)/shard_map/ppermute | solution.py:207
  33.8 2.1 %collective-permute-done.10 = bf16[32,1024]{1,0:T(8,128)(2,1)S(1)} collective-permute-done((bf16[32,1024]{1,0:T(8,128)(2,1)S(1)}, bf16[32,1024]{1,0:T(8,128)(2,1)S(1)}, u32[]{:S(2)}, u32[]{:S(2)}) %collective-permute-start.10) | collective-permute-done | bytes 65568 | tf_op jit(solution)/shard_map/ppermute | solution.py:207
  35.9 2.7 %collective-permute-done.9 = bf16[32,1024]{1,0:T(8,128)(2,1)S(1)} collective-permute-done((bf16[32,1024]{1,0:T(8,128)(2,1)S(1)}, bf16[32,1024]{1,0:T(8,128)(2,1)S(1)}, u32[]{:S(2)}, u32[]{:S(2)}) %collective-permute-start.9) | collective-permute-done | bytes 65568 | tf_op jit(solution)/shard_map/ppermute | solution.py:207
  38.6 0.0 collective-permute-done.8
  38.6 0.0 copy-start.1
  38.6 0.1 collective-permute-start.11
  38.7 1.2 %collective-permute-done.11.other_ref = bf16[32,1024]{1,0:T(8,128)(2,1)S(1)} collective-permute-done((bf16[32,1024]{1,0:T(8,128)(2,1)S(1)}, bf16[32,1024]{1,0:T(8,128)(2,1)S(1)}, u32[]{:S(2)}, u32[]{:S(2)}) %collective-permute-start.11) | collective-permute-done | bytes 65568 | tf_op jit(solution)/shard_map/ppermute | solution.py:207
  40.0 0.0 copy-done.1
  40.0 0.0 copy-start.5
  40.0 0.6 %copy-done.5 = bf16[32,1024]{1,0:T(8,128)(2,1)} copy-done((bf16[32,1024]{1,0:T(8,128)(2,1)}, bf16[32,1024]{1,0:T(8,128)(2,1)S(1)}, u32[]{:S(2)}) %copy-start.5) | copy-done | bytes 65560
  40.6 1.6 %join.1 = (f32[32,108]{1,0:T(8,128)}, f32[64,864]{1,0:T(8,128)}) custom-call(bf16[32,1024]{1,0:T(8,128)(2,1)} %copy-done.1, bf16[32,1024]{1,0:T(8,128)(2,1)} %copy-done.5), custom_call_target="tpu_custom_call" | custom-call | tf_op jit(solution)/shard_map/join/pallas_call | solution.py:283
  (10 shorter events, 0.2 us)
Async XLA Ops:
  0.6 0.8 %copy-start.2 = (bf16[1,4,4,8,128]{4,3,2,1,0:T(8,128)(2,1)S(1)}, bf16[1,4,4,8,128]{4,3,2,1,0:T(8,128)(2,1)}, u32[]{:S(2)}) copy-start(bf16[1,4,4,8,128]{4,3,2,1,0:T(8,128)(2,1)} %param.4) | copy-start | bytes 98308
  1.4 1.4 %collective-permute-start = (bf16[3,32,128]{2,1,0:T(8,128)(2,1)S(1)}, bf16[3,32,128]{2,1,0:T(8,128)(2,1)S(1)}, u32[]{:S(2)}, u32[]{:S(2)}) collective-permute-start(bf16[3,32,128]{2,1,0:T(8,128)(2,1)S(1)} %bitcast.12), channel_id=1, source_target_pairs={{0,2},{2,0},{4,6},{6,4},{1,3},{3,1},{5,7},{7,5},{8,10},{10,8},{12,... | collective-permute-start | bytes 73736 | tf_op jit(solution)/shard_map/ppermute | solution.py:207
  2.0 5.0 %copy-start.3 = (bf16[1,64,2,4,64]{4,3,2,1,0:T(4,128)(2,1)S(1)}, bf16[1,64,2,4,64]{4,3,2,1,0:T(4,128)(2,1)}, u32[]{:S(2)}) copy-start(bf16[1,64,2,4,64]{4,3,2,1,0:T(4,128)(2,1)} %param.7) | copy-start | bytes 196612
  2.0 5.7 %collective-permute-start.1 = (bf16[3,32,128]{2,1,0:T(8,128)(2,1)S(1)}, bf16[3,32,128]{2,1,0:T(8,128)(2,1)S(1)}, u32[]{:S(2)}, u32[]{:S(2)}) collective-permute-start(bf16[3,32,128]{2,1,0:T(8,128)(2,1)S(1)} %bitcast.10), channel_id=1, source_target_pairs={{2,4},{4,2},{3,5},{5,3},{10,12},{12,10},{11,13},{13,11},{18,20},{2... | collective-permute-start | bytes 73736 | tf_op jit(solution)/shard_map/ppermute | solution.py:254
  2.8 0.6 %copy-start = (bf16[4,8,4,128]{3,2,1,0:T(4,128)(2,1)}, bf16[4,8,4,128]{3,2,1,0:T(4,128)(2,1)S(1)}, u32[]{:S(2)}) copy-start(bf16[4,8,4,128]{3,2,1,0:T(4,128)(2,1)S(1)} %copy.6) | copy-start | bytes 98308
  2.9 0.6 %copy-start.4 = (bf16[3,32,128]{2,1,0:T(8,128)(2,1)}, bf16[3,32,128]{2,1,0:T(8,128)(2,1)S(1)}, u32[]{:S(2)}) copy-start(bf16[3,32,128]{2,1,0:T(8,128)(2,1)S(1)} %collective-permute-done.near_ref) | copy-start | bytes 73732
  3.5 4.6 %collective-permute-start.2 = (bf16[7,12,128]{2,1,0:T(8,128)(2,1)S(1)}, bf16[7,12,128]{2,1,0:T(8,128)(2,1)S(1)}, u32[]{:S(2)}, u32[]{:S(2)}) collective-permute-start(bf16[7,12,128]{2,1,0:T(8,128)(2,1)S(1)} %pad_maximum_fusion), channel_id=1, source_target_pairs={{0,1},{1,0},{2,3},{3,2},{4,5},{5,4},{6,7},{7,6},{8,9},{9,8},{10,11... | collective-permute-start | bytes 64520 | tf_op jit(solution)/shard_map/ppermute | solution.py:207
  6.3 1.5 %collective-permute-start.3 = (bf16[3,12,128]{2,1,0:T(8,128)(2,1)S(1)}, bf16[3,12,128]{2,1,0:T(8,128)(2,1)S(1)}, u32[]{:S(2)}, u32[]{:S(2)}) collective-permute-start(bf16[3,12,128]{2,1,0:T(8,128)(2,1)S(1)} %slice_select_fusion.1), channel_id=1, source_target_pairs={{2,5},{3,4},{4,3},{5,2},{10,13},{11,12},{12,11},{13,10},{18,21},{1... | collective-permute-start | bytes 27656 | tf_op jit(solution)/shard_map/ppermute | solution.py:256
  7.7 0.6 %copy-start.8 = (bf16[3,12,128]{2,1,0:T(8,128)(2,1)}, bf16[3,12,128]{2,1,0:T(8,128)(2,1)S(1)}, u32[]{:S(2)}) copy-start(bf16[3,12,128]{2,1,0:T(8,128)(2,1)S(1)} %collective-permute-done.3.diag_ref) | copy-start | bytes 27652
  7.7 0.6 %copy-start.7 = (bf16[3,32,128]{2,1,0:T(8,128)(2,1)}, bf16[3,32,128]{2,1,0:T(8,128)(2,1)S(1)}, u32[]{:S(2)}) copy-start(bf16[3,32,128]{2,1,0:T(8,128)(2,1)S(1)} %collective-permute-done.1.far_ref) | copy-start | bytes 73732
  8.3 0.6 %copy-start.6 = (bf16[7,12,128]{2,1,0:T(8,128)(2,1)}, bf16[7,12,128]{2,1,0:T(8,128)(2,1)S(1)}, u32[]{:S(2)}) copy-start(bf16[7,12,128]{2,1,0:T(8,128)(2,1)S(1)} %collective-permute-done.2.side_ref) | copy-start | bytes 64516
  14.1 7.9 %collective-permute-start.4 = (bf16[32,1024]{1,0:T(8,128)(2,1)}, bf16[32,1024]{1,0:T(8,128)(2,1)S(1)}, u32[]{:S(2)}, u32[]{:S(2)}) collective-permute-start(bf16[32,1024]{1,0:T(8,128)(2,1)} %get-tuple-element.5), channel_id=1, source_target_pairs={{0,2},{2,0},{4,6},{6,4},{1,3},{3,1},{5,7},{7,5},{8,10},{10,8},{12,... | collective-permute-start | bytes 196616 | tf_op jit(solution)/shard_map/ppermute | solution.py:207
  22.9 5.9 %collective-permute-start.7 = (bf16[32,1024]{1,0:T(8,128)(2,1)S(1)}, bf16[32,1024]{1,0:T(8,128)(2,1)S(1)}, u32[]{:S(2)}, u32[]{:S(2)}) collective-permute-start(bf16[32,1024]{1,0:T(8,128)(2,1)S(1)} %add_convert_fusion.2), channel_id=1, source_target_pairs={{0,5},{1,4},{2,7},{3,6},{4,1},{5,0},{6,3},{7,2},{8,13},{9,12},{10,... | collective-permute-start | bytes 196616 | tf_op jit(solution)/shard_map/ppermute | solution.py:207
  23.6 5.4 %collective-permute-start.6 = (bf16[32,1024]{1,0:T(8,128)(2,1)S(1)}, bf16[32,1024]{1,0:T(8,128)(2,1)S(1)}, u32[]{:S(2)}, u32[]{:S(2)}) collective-permute-start(bf16[32,1024]{1,0:T(8,128)(2,1)S(1)} %add_convert_fusion.2), channel_id=1, source_target_pairs={{0,4},{1,5},{2,6},{3,7},{4,0},{5,1},{6,2},{7,3},{8,12},{9,13},{10,... | collective-permute-start | bytes 196616 | tf_op jit(solution)/shard_map/ppermute | solution.py:207
  25.0 4.3 %collective-permute-start.5 = (bf16[32,1024]{1,0:T(8,128)(2,1)S(1)}, bf16[32,1024]{1,0:T(8,128)(2,1)S(1)}, u32[]{:S(2)}, u32[]{:S(2)}) collective-permute-start(bf16[32,1024]{1,0:T(8,128)(2,1)S(1)} %add_convert_fusion.2), channel_id=1, source_target_pairs={{0,1},{1,0},{2,3},{3,2},{4,5},{5,4},{6,7},{7,6},{8,9},{9,8},{10,11... | collective-permute-start | bytes 196616 | tf_op jit(solution)/shard_map/ppermute | solution.py:207
  29.3 6.5 %collective-permute-start.10 = (bf16[32,1024]{1,0:T(8,128)(2,1)S(1)}, bf16[32,1024]{1,0:T(8,128)(2,1)S(1)}, u32[]{:S(2)}, u32[]{:S(2)}) collective-permute-start(bf16[32,1024]{1,0:T(8,128)(2,1)S(1)} %add_convert_fusion.1), channel_id=1, source_target_pairs={{0,24},{8,16},{16,8},{24,0},{1,25},{9,17},{17,9},{25,1},{2,26},{10... | collective-permute-start | bytes 196616 | tf_op jit(solution)/shard_map/ppermute | solution.py:207
  33.1 5.5 %collective-permute-start.9 = (bf16[32,1024]{1,0:T(8,128)(2,1)S(1)}, bf16[32,1024]{1,0:T(8,128)(2,1)S(1)}, u32[]{:S(2)}, u32[]{:S(2)}) collective-permute-start(bf16[32,1024]{1,0:T(8,128)(2,1)S(1)} %add_convert_fusion.1), channel_id=1, source_target_pairs={{0,16},{8,24},{16,0},{24,8},{1,17},{9,25},{17,1},{25,9},{2,18},{10... | collective-permute-start | bytes 196616 | tf_op jit(solution)/shard_map/ppermute | solution.py:207
  33.1 5.5 %collective-permute-start.8 = (bf16[32,1024]{1,0:T(8,128)(2,1)S(1)}, bf16[32,1024]{1,0:T(8,128)(2,1)S(1)}, u32[]{:S(2)}, u32[]{:S(2)}) collective-permute-start(bf16[32,1024]{1,0:T(8,128)(2,1)S(1)} %add_convert_fusion.1), channel_id=1, source_target_pairs={{0,8},{8,0},{16,24},{24,16},{1,9},{9,1},{17,25},{25,17},{2,10},{10... | collective-permute-start | bytes 196616 | tf_op jit(solution)/shard_map/ppermute | solution.py:207
  38.6 1.3 %copy-start.1 = (bf16[32,1024]{1,0:T(8,128)(2,1)}, bf16[32,1024]{1,0:T(8,128)(2,1)S(1)}, u32[]{:S(2)}) copy-start(bf16[32,1024]{1,0:T(8,128)(2,1)S(1)} %add_convert_fusion.mine_ref) | copy-start | bytes 196612
  38.6 1.3 %collective-permute-start.11 = (bf16[32,1024]{1,0:T(8,128)(2,1)S(1)}, bf16[32,1024]{1,0:T(8,128)(2,1)S(1)}, u32[]{:S(2)}, u32[]{:S(2)}) collective-permute-start(bf16[32,1024]{1,0:T(8,128)(2,1)S(1)} %add_convert_fusion.mine_ref), channel_id=1, source_target_pairs={{0,2},{2,0},{4,6},{6,4},{1,3},{3,1},{5,7},{7,5},{8,10},{10,8},{12,... | collective-permute-start | bytes 196616 | tf_op jit(solution)/shard_map/ppermute | solution.py:207
  40.0 0.6 %copy-start.5 = (bf16[32,1024]{1,0:T(8,128)(2,1)}, bf16[32,1024]{1,0:T(8,128)(2,1)S(1)}, u32[]{:S(2)}) copy-start(bf16[32,1024]{1,0:T(8,128)(2,1)S(1)} %collective-permute-done.11.other_ref) | copy-start | bytes 196612

commit v3 on v2

--- a/solution.py
+++ b/solution.py
@@ -219,6 +219,10 @@
     return value
 
 
+def near_core(value):
+    return pltpu.with_memory_space_constraint(value, pltpu.VMEM)
+
+
 def bits(count):
     return [1 << i for i in range(count.bit_length() - 1)]
 
@@ -264,8 +268,8 @@
     keep, send = pl.pallas_call(
         body,
         out_shape=(
-            jax.ShapeDtypeStruct((c2 // 2, width), F32),
-            jax.ShapeDtypeStruct((c2 // 2, width), BF16),
+            pltpu.VMEM((c2 // 2, width), F32),
+            pltpu.VMEM((c2 // 2, width), BF16),
         ),
         scratch_shapes=[
             pltpu.VMEM((wx + 2 * RIM, (wy + 2 * RIM) * cin, wz), F32),
@@ -276,7 +280,7 @@
             pltpu.VMEM((8 * c1, lane), BF16),
         ],
         name="local_step",
-    )(block, near, far, side, diag, first_weight, second_weight, cot)
+    )(*map(near_core, (block, near, far, side, diag)), first_weight, second_weight, near_core(cot))
     mine = (keep + swap(send, "sx", 1).astype(F32)).astype(BF16)
     mine = total_over(mine, ("sx", "sy"), [1] + [2 * m for m in bits(count_x)[1:]])
     mine = total_over(mine, ("dp",), bits(lax.axis_size("dp")))
@@ -287,7 +291,7 @@
             jax.ShapeDtypeStruct((c2, tall), F32),
         ),
         name="join",
-    )(mine, swap(mine, "sx", 1))
+    )(near_core(mine), near_core(swap(mine, "sx", 1)))
 
 
 def solution(mesh):

time: 42.5 us -> 37.3 us (0.88)
  local copies, waits for them, and re-layouts: 3.61 us -> 0.93 us
  Pallas kernels: 6.73 us -> 5.09 us
  other arithmetic: 1.04 us -> 0.14 us
    unnamed x18 -> x4, local copies, waits for them, and re-layouts: 2.8 us -> 0.74 us
    convert_element_type x1, other arithmetic: 0.92 us -> 0.02 us  [shards(): mine = (keep + swap(send, 'sx', 1).astype(F32)).astype(BF16)]
    pallas_call x1, Pallas kernels: 1.58 us -> 0.71 us  [shards(): pl.pallas_call(functools.partial(join_kernel, g_lane=g_lane), out_shape=(...]
    pallas_call x1, Pallas kernels: 5.14 us -> 4.37 us  [shards(): pl.pallas_call(body, out_shape=(pltpu.VMEM((c2 // 2, width), F32), pltpu....]
    another operation x1, local copies, waits for them, and re-layouts: 0.77 us -> 0.14 us  [shards(): cot = cotangent[0].reshape(c2, hx * hy * hz)]
  transfers between devices with their start and end apart: 12 -> 12, of which waited for: 8 -> 8; matrix products, arithmetic and copies ran while one was open for 2% -> 1% of each run, Pallas kernels for 0% -> 0%
where the time goes in v3:
time: 37.3 us; the launch traced here: 37.1 us
  starting transfers between devices  19.4 us (52%)
  waiting for transfers between devices  10.7 us (29%)
  Pallas kernels  5.09 us (14%)
  local copies, waits for them, and re-layouts  0.93 us (2%)
  between operations  0.8 us (2%)
    ppermute x10, starting transfers between devices, swap(): return lax.ppermute(value, axes, [(i, i ^ mask) for i in range(count)])  17.9 us
    ppermute x10, waiting for transfers between devices, swap(): return lax.ppermute(value, axes, [(i, i ^ mask) for i in range(count)])  10.7 us
    pallas_call x1, Pallas kernels, shards(): pl.pallas_call(body, out_shape=(pltpu.VMEM((c2 // 2, width), F32), pltpu....  4.37 us
    ppermute x1, starting transfers between devices, shards(): far = lax.ppermute(outer, 'sx', pairs)  0.79 us
  transfers between devices with their start and end apart: 12, of which 8 were waited for; matrix products, arithmetic and copies ran while one was open for 1% of the time, Pallas kernels for 0%

profile of v3, /device:TPU:0, one launch (start us, length us, event | category | flops | bytes accessed | tf_op | source)
XLA Modules:
  0.0 37.1 jit_solution(1958038557725677545)
XLA Ops:
  0.6 0.0 copy-start
  0.7 0.7 %copy-done = bf16[1,4,4,8,128]{4,3,2,1,0:T(8,128)(2,1)S(1)} copy-done((bf16[1,4,4,8,128]{4,3,2,1,0:T(8,128)(2,1)S(1)}, bf16[1,4,4,8,128]{4,3,2,1,0:T(8,128)(2,1)}, u32[]{:S(2)}) %copy-start) | copy-done | bytes 32792
  1.4 0.6 %collective-permute-start = (bf16[3,32,128]{2,1,0:T(8,128)(2,1)S(1)}, bf16[3,32,128]{2,1,0:T(8,128)(2,1)S(1)}, u32[]{:S(2)}, u32[]{:S(2)}) collective-permute-start(bf16[3,32,128]{2,1,0:T(8,128)(2,1)S(1)} %bitcast.12), channel_id=1, source_target_pairs={{0,2},{2,0},{4,6},{6,4},{1,3},{3,1},{5,7},{7,5},{8,10},{10,8},{12,... | collective-permute-start | bytes 73736 | tf_op jit(solution)/shard_map/ppermute | solution.py:207
  2.0 0.0 copy-start.1
  2.0 0.8 %collective-permute-start.1 = (bf16[3,32,128]{2,1,0:T(8,128)(2,1)S(1)}, bf16[3,32,128]{2,1,0:T(8,128)(2,1)S(1)}, u32[]{:S(2)}, u32[]{:S(2)}) collective-permute-start(bf16[3,32,128]{2,1,0:T(8,128)(2,1)S(1)} %bitcast.10), channel_id=1, source_target_pairs={{2,4},{4,2},{3,5},{5,3},{10,12},{12,10},{11,13},{13,11},{18,20},{2... | collective-permute-start | bytes 73736 | tf_op jit(solution)/shard_map/ppermute | solution.py:258
  2.9 0.0 collective-permute-done.near_ref
  2.9 2.8 %collective-permute-start.2 = (bf16[7,12,128]{2,1,0:T(8,128)(2,1)S(1)}, bf16[7,12,128]{2,1,0:T(8,128)(2,1)S(1)}, u32[]{:S(2)}, u32[]{:S(2)}) collective-permute-start(bf16[7,12,128]{2,1,0:T(8,128)(2,1)S(1)} %pad_maximum_fusion), channel_id=1, source_target_pairs={{0,1},{1,0},{2,3},{3,2},{4,5},{5,4},{6,7},{7,6},{8,9},{9,8},{10,11... | collective-permute-start | bytes 64520 | tf_op jit(solution)/shard_map/ppermute | solution.py:207
  5.8 0.7 %collective-permute-start.3 = (bf16[3,12,128]{2,1,0:T(8,128)(2,1)S(1)}, bf16[3,12,128]{2,1,0:T(8,128)(2,1)S(1)}, u32[]{:S(2)}, u32[]{:S(2)}) collective-permute-start(bf16[3,12,128]{2,1,0:T(8,128)(2,1)S(1)} %slice_select_fusion.1), channel_id=1, source_target_pairs={{2,5},{3,4},{4,3},{5,2},{10,13},{11,12},{12,11},{13,10},{18,21},{1... | collective-permute-start | bytes 27656 | tf_op jit(solution)/shard_map/ppermute | solution.py:260
  6.4 0.0 copy-done.1
  6.4 0.1 reshape_squeeze.3.cot_ref
  6.6 0.0 collective-permute-done.3.diag_ref
  6.6 0.0 collective-permute-done.1.far_ref
  6.6 1.0 %collective-permute-done.2.side_ref = bf16[7,12,128]{2,1,0:T(8,128)(2,1)S(1)} collective-permute-done((bf16[7,12,128]{2,1,0:T(8,128)(2,1)S(1)}, bf16[7,12,128]{2,1,0:T(8,128)(2,1)S(1)}, u32[]{:S(2)}, u32[]{:S(2)}) %collective-permute-start.2) | collective-permute-done | bytes 21536 | tf_op jit(solution)/shard_map/ppermute | solution.py:207
  7.6 4.4 %local_step.1 = (f32[32,1024]{1,0:T(8,128)S(1)}, bf16[32,1024]{1,0:T(8,128)(2,1)S(1)}) custom-call(bf16[4,32,128]{2,1,0:T(8,128)(2,1)S(1)} %bitcast.7, bf16[3,32,128]{2,1,0:T(8,128)(2,1)S(1)} %collective-permute-done.near_ref, bf16[3,32,128]{2,1,0:T(8,128)(2,1)S(1)} %collective-permute-done.1.far_ref, ...), custom_call_target="tpu_custom_call" | custom-call | tf_op jit(solution)/shard_map/local_step/pallas_call | solution.py:268
  12.0 6.5 %collective-permute-start.4 = (bf16[32,1024]{1,0:T(8,128)(2,1)S(1)}, bf16[32,1024]{1,0:T(8,128)(2,1)S(1)}, u32[]{:S(2)}, u32[]{:S(2)}) collective-permute-start(bf16[32,1024]{1,0:T(8,128)(2,1)S(1)} %get-tuple-element.5), channel_id=1, source_target_pairs={{0,2},{2,0},{4,6},{6,4},{1,3},{3,1},{5,7},{7,5},{8,10},{10,8},{12,... | collective-permute-start | bytes 196616 | tf_op jit(solution)/shard_map/ppermute | solution.py:207
  18.4 0.9 %collective-permute-done.4 = bf16[32,1024]{1,0:T(8,128)(2,1)S(1)} collective-permute-done((bf16[32,1024]{1,0:T(8,128)(2,1)S(1)}, bf16[32,1024]{1,0:T(8,128)(2,1)S(1)}, u32[]{:S(2)}, u32[]{:S(2)}) %collective-permute-start.4) | collective-permute-done | bytes 65568 | tf_op jit(solution)/shard_map/ppermute | solution.py:207
  19.4 0.6 %collective-permute-start.7 = (bf16[32,1024]{1,0:T(8,128)(2,1)S(1)}, bf16[32,1024]{1,0:T(8,128)(2,1)S(1)}, u32[]{:S(2)}, u32[]{:S(2)}) collective-permute-start(bf16[32,1024]{1,0:T(8,128)(2,1)S(1)} %add_convert_fusion.2), channel_id=1, source_target_pairs={{0,5},{1,4},{2,7},{3,6},{4,1},{5,0},{6,3},{7,2},{8,13},{9,12},{10,... | collective-permute-start | bytes 196616 | tf_op jit(solution)/shard_map/ppermute | solution.py:207
  20.0 1.4 %collective-permute-start.6 = (bf16[32,1024]{1,0:T(8,128)(2,1)S(1)}, bf16[32,1024]{1,0:T(8,128)(2,1)S(1)}, u32[]{:S(2)}, u32[]{:S(2)}) collective-permute-start(bf16[32,1024]{1,0:T(8,128)(2,1)S(1)} %add_convert_fusion.2), channel_id=1, source_target_pairs={{0,4},{1,5},{2,6},{3,7},{4,0},{5,1},{6,2},{7,3},{8,12},{9,13},{10,... | collective-permute-start | bytes 196616 | tf_op jit(solution)/shard_map/ppermute | solution.py:207
  21.4 1.5 %collective-permute-start.5 = (bf16[32,1024]{1,0:T(8,128)(2,1)S(1)}, bf16[32,1024]{1,0:T(8,128)(2,1)S(1)}, u32[]{:S(2)}, u32[]{:S(2)}) collective-permute-start(bf16[32,1024]{1,0:T(8,128)(2,1)S(1)} %add_convert_fusion.2), channel_id=1, source_target_pairs={{0,1},{1,0},{2,3},{3,2},{4,5},{5,4},{6,7},{7,6},{8,9},{9,8},{10,11... | collective-permute-start | bytes 196616 | tf_op jit(solution)/shard_map/ppermute | solution.py:207
  22.9 2.4 %collective-permute-done.7 = bf16[32,1024]{1,0:T(8,128)(2,1)S(1)} collective-permute-done((bf16[32,1024]{1,0:T(8,128)(2,1)S(1)}, bf16[32,1024]{1,0:T(8,128)(2,1)S(1)}, u32[]{:S(2)}, u32[]{:S(2)}) %collective-permute-start.7) | collective-permute-done | bytes 65568 | tf_op jit(solution)/shard_map/ppermute | solution.py:207
  25.3 0.1 collective-permute-done.6
  25.4 0.3 collective-permute-done.5
  25.7 3.8 %collective-permute-start.10 = (bf16[32,1024]{1,0:T(8,128)(2,1)S(1)}, bf16[32,1024]{1,0:T(8,128)(2,1)S(1)}, u32[]{:S(2)}, u32[]{:S(2)}) collective-permute-start(bf16[32,1024]{1,0:T(8,128)(2,1)S(1)} %add_convert_fusion.1), channel_id=1, source_target_pairs={{0,24},{8,16},{16,8},{24,0},{1,25},{9,17},{17,9},{25,1},{2,26},{10... | collective-permute-start | bytes 196616 | tf_op jit(solution)/shard_map/ppermute | solution.py:207
  29.5 0.0 collective-permute-start.9
  29.5 0.7 %collective-permute-start.8 = (bf16[32,1024]{1,0:T(8,128)(2,1)S(1)}, bf16[32,1024]{1,0:T(8,128)(2,1)S(1)}, u32[]{:S(2)}, u32[]{:S(2)}) collective-permute-start(bf16[32,1024]{1,0:T(8,128)(2,1)S(1)} %add_convert_fusion.1), channel_id=1, source_target_pairs={{0,8},{8,0},{16,24},{24,16},{1,9},{9,1},{17,25},{25,17},{2,10},{10... | collective-permute-start | bytes 196616 | tf_op jit(solution)/shard_map/ppermute | solution.py:207
  30.2 2.1 %collective-permute-done.10 = bf16[32,1024]{1,0:T(8,128)(2,1)S(1)} collective-permute-done((bf16[32,1024]{1,0:T(8,128)(2,1)S(1)}, bf16[32,1024]{1,0:T(8,128)(2,1)S(1)}, u32[]{:S(2)}, u32[]{:S(2)}) %collective-permute-start.10) | collective-permute-done | bytes 65568 | tf_op jit(solution)/shard_map/ppermute | solution.py:207
  32.3 2.7 %collective-permute-done.9 = bf16[32,1024]{1,0:T(8,128)(2,1)S(1)} collective-permute-done((bf16[32,1024]{1,0:T(8,128)(2,1)S(1)}, bf16[32,1024]{1,0:T(8,128)(2,1)S(1)}, u32[]{:S(2)}, u32[]{:S(2)}) %collective-permute-start.9) | collective-permute-done | bytes 65568 | tf_op jit(solution)/shard_map/ppermute | solution.py:207
  35.0 0.0 collective-permute-done.8
  35.1 0.1 collective-permute-start.11
  35.1 1.2 %collective-permute-done.11.other_ref = bf16[32,1024]{1,0:T(8,128)(2,1)S(1)} collective-permute-done((bf16[32,1024]{1,0:T(8,128)(2,1)S(1)}, bf16[32,1024]{1,0:T(8,128)(2,1)S(1)}, u32[]{:S(2)}, u32[]{:S(2)}) %collective-permute-start.11) | collective-permute-done | bytes 65568 | tf_op jit(solution)/shard_map/ppermute | solution.py:207
  36.4 0.7 %join.1 = (f32[32,108]{1,0:T(8,128)}, f32[64,864]{1,0:T(8,128)}) custom-call(bf16[32,1024]{1,0:T(8,128)(2,1)S(1)} %add_convert_fusion.mine_ref, bf16[32,1024]{1,0:T(8,128)(2,1)S(1)} %collective-permute-done.11.other_ref), custom_call_target="tpu_custom_call" | custom-call | tf_op jit(solution)/shard_map/join/pallas_call | solution.py:287
  (11 shorter events, 0.2 us)
Async XLA Ops:
  0.6 0.8 %copy-start = (bf16[1,4,4,8,128]{4,3,2,1,0:T(8,128)(2,1)S(1)}, bf16[1,4,4,8,128]{4,3,2,1,0:T(8,128)(2,1)}, u32[]{:S(2)}) copy-start(bf16[1,4,4,8,128]{4,3,2,1,0:T(8,128)(2,1)} %param.4) | copy-start | bytes 98308
  1.4 1.4 %collective-permute-start = (bf16[3,32,128]{2,1,0:T(8,128)(2,1)S(1)}, bf16[3,32,128]{2,1,0:T(8,128)(2,1)S(1)}, u32[]{:S(2)}, u32[]{:S(2)}) collective-permute-start(bf16[3,32,128]{2,1,0:T(8,128)(2,1)S(1)} %bitcast.12), channel_id=1, source_target_pairs={{0,2},{2,0},{4,6},{6,4},{1,3},{3,1},{5,7},{7,5},{8,10},{10,8},{12,... | collective-permute-start | bytes 73736 | tf_op jit(solution)/shard_map/ppermute | solution.py:207
  2.0 4.4 %copy-start.1 = (bf16[1,64,2,4,64]{4,3,2,1,0:T(4,128)(2,1)S(1)}, bf16[1,64,2,4,64]{4,3,2,1,0:T(4,128)(2,1)}, u32[]{:S(2)}) copy-start(bf16[1,64,2,4,64]{4,3,2,1,0:T(4,128)(2,1)} %param.7) | copy-start | bytes 196612
  2.0 4.6 %collective-permute-start.1 = (bf16[3,32,128]{2,1,0:T(8,128)(2,1)S(1)}, bf16[3,32,128]{2,1,0:T(8,128)(2,1)S(1)}, u32[]{:S(2)}, u32[]{:S(2)}) collective-permute-start(bf16[3,32,128]{2,1,0:T(8,128)(2,1)S(1)} %bitcast.10), channel_id=1, source_target_pairs={{2,4},{4,2},{3,5},{5,3},{10,12},{12,10},{11,13},{13,11},{18,20},{2... | collective-permute-start | bytes 73736 | tf_op jit(solution)/shard_map/ppermute | solution.py:258
  2.9 4.7 %collective-permute-start.2 = (bf16[7,12,128]{2,1,0:T(8,128)(2,1)S(1)}, bf16[7,12,128]{2,1,0:T(8,128)(2,1)S(1)}, u32[]{:S(2)}, u32[]{:S(2)}) collective-permute-start(bf16[7,12,128]{2,1,0:T(8,128)(2,1)S(1)} %pad_maximum_fusion), channel_id=1, source_target_pairs={{0,1},{1,0},{2,3},{3,2},{4,5},{5,4},{6,7},{7,6},{8,9},{9,8},{10,11... | collective-permute-start | bytes 64520 | tf_op jit(solution)/shard_map/ppermute | solution.py:207
  5.8 0.8 %collective-permute-start.3 = (bf16[3,12,128]{2,1,0:T(8,128)(2,1)S(1)}, bf16[3,12,128]{2,1,0:T(8,128)(2,1)S(1)}, u32[]{:S(2)}, u32[]{:S(2)}) collective-permute-start(bf16[3,12,128]{2,1,0:T(8,128)(2,1)S(1)} %slice_select_fusion.1), channel_id=1, source_target_pairs={{2,5},{3,4},{4,3},{5,2},{10,13},{11,12},{12,11},{13,10},{18,21},{1... | collective-permute-start | bytes 27656 | tf_op jit(solution)/shard_map/ppermute | solution.py:260
  12.0 7.4 %collective-permute-start.4 = (bf16[32,1024]{1,0:T(8,128)(2,1)S(1)}, bf16[32,1024]{1,0:T(8,128)(2,1)S(1)}, u32[]{:S(2)}, u32[]{:S(2)}) collective-permute-start(bf16[32,1024]{1,0:T(8,128)(2,1)S(1)} %get-tuple-element.5), channel_id=1, source_target_pairs={{0,2},{2,0},{4,6},{6,4},{1,3},{3,1},{5,7},{7,5},{8,10},{10,8},{12,... | collective-permute-start | bytes 196616 | tf_op jit(solution)/shard_map/ppermute | solution.py:207
  19.4 5.9 %collective-permute-start.7 = (bf16[32,1024]{1,0:T(8,128)(2,1)S(1)}, bf16[32,1024]{1,0:T(8,128)(2,1)S(1)}, u32[]{:S(2)}, u32[]{:S(2)}) collective-permute-start(bf16[32,1024]{1,0:T(8,128)(2,1)S(1)} %add_convert_fusion.2), channel_id=1, source_target_pairs={{0,5},{1,4},{2,7},{3,6},{4,1},{5,0},{6,3},{7,2},{8,13},{9,12},{10,... | collective-permute-start | bytes 196616 | tf_op jit(solution)/shard_map/ppermute | solution.py:207
  20.0 5.4 %collective-permute-start.6 = (bf16[32,1024]{1,0:T(8,128)(2,1)S(1)}, bf16[32,1024]{1,0:T(8,128)(2,1)S(1)}, u32[]{:S(2)}, u32[]{:S(2)}) collective-permute-start(bf16[32,1024]{1,0:T(8,128)(2,1)S(1)} %add_convert_fusion.2), channel_id=1, source_target_pairs={{0,4},{1,5},{2,6},{3,7},{4,0},{5,1},{6,2},{7,3},{8,12},{9,13},{10,... | collective-permute-start | bytes 196616 | tf_op jit(solution)/shard_map/ppermute | solution.py:207
  21.4 4.3 %collective-permute-start.5 = (bf16[32,1024]{1,0:T(8,128)(2,1)S(1)}, bf16[32,1024]{1,0:T(8,128)(2,1)S(1)}, u32[]{:S(2)}, u32[]{:S(2)}) collective-permute-start(bf16[32,1024]{1,0:T(8,128)(2,1)S(1)} %add_convert_fusion.2), channel_id=1, source_target_pairs={{0,1},{1,0},{2,3},{3,2},{4,5},{5,4},{6,7},{7,6},{8,9},{9,8},{10,11... | collective-permute-start | bytes 196616 | tf_op jit(solution)/shard_map/ppermute | solution.py:207
  25.7 6.6 %collective-permute-start.10 = (bf16[32,1024]{1,0:T(8,128)(2,1)S(1)}, bf16[32,1024]{1,0:T(8,128)(2,1)S(1)}, u32[]{:S(2)}, u32[]{:S(2)}) collective-permute-start(bf16[32,1024]{1,0:T(8,128)(2,1)S(1)} %add_convert_fusion.1), channel_id=1, source_target_pairs={{0,24},{8,16},{16,8},{24,0},{1,25},{9,17},{17,9},{25,1},{2,26},{10... | collective-permute-start | bytes 196616 | tf_op jit(solution)/shard_map/ppermute | solution.py:207
  29.5 5.5 %collective-permute-start.9 = (bf16[32,1024]{1,0:T(8,128)(2,1)S(1)}, bf16[32,1024]{1,0:T(8,128)(2,1)S(1)}, u32[]{:S(2)}, u32[]{:S(2)}) collective-permute-start(bf16[32,1024]{1,0:T(8,128)(2,1)S(1)} %add_convert_fusion.1), channel_id=1, source_target_pairs={{0,16},{8,24},{16,0},{24,8},{1,17},{9,25},{17,1},{25,9},{2,18},{10... | collective-permute-start | bytes 196616 | tf_op jit(solution)/shard_map/ppermute | solution.py:207
  29.5 5.5 %collective-permute-start.8 = (bf16[32,1024]{1,0:T(8,128)(2,1)S(1)}, bf16[32,1024]{1,0:T(8,128)(2,1)S(1)}, u32[]{:S(2)}, u32[]{:S(2)}) collective-permute-start(bf16[32,1024]{1,0:T(8,128)(2,1)S(1)} %add_convert_fusion.1), channel_id=1, source_target_pairs={{0,8},{8,0},{16,24},{24,16},{1,9},{9,1},{17,25},{25,17},{2,10},{10... | collective-permute-start | bytes 196616 | tf_op jit(solution)/shard_map/ppermute | solution.py:207
  35.1 1.3 %collective-permute-start.11 = (bf16[32,1024]{1,0:T(8,128)(2,1)S(1)}, bf16[32,1024]{1,0:T(8,128)(2,1)S(1)}, u32[]{:S(2)}, u32[]{:S(2)}) collective-permute-start(bf16[32,1024]{1,0:T(8,128)(2,1)S(1)} %add_convert_fusion.mine_ref), channel_id=1, source_target_pairs={{0,2},{2,0},{4,6},{6,4},{1,3},{3,1},{5,7},{7,5},{8,10},{10,8},{12,... | collective-permute-start | bytes 196616 | tf_op jit(solution)/shard_map/ppermute | solution.py:207

commit v4 on v3

--- a/solution.py
+++ b/solution.py
@@ -24,7 +24,7 @@
 
 
 def local_kernel(
-    block_ref, near_ref, far_ref, side_ref, diag_ref, w1_ref, w2_ref, cot_ref, keep_ref, send_ref,
+    block_ref, near_ref, far_ref, side_ref, w1_ref, w2_ref, cot_ref, keep_ref, send_ref,
     vf, lhs, s_ref, slope_ref, cols, lower,
     *, cin, hx, hy, hz, g_lane, scale_first, scale_second,
 ):
@@ -43,12 +43,12 @@
     near_at = jnp.where(odd_x == 1, 0, RIM + wx)
     far_at = RIM + wx - near_at
     vf[RIM : RIM + wx, lip : lip + rows, :] = block_ref[...].astype(F32)
-    vf[pl.ds(near_at, RIM), lip : lip + rows, :] = near_ref[...].astype(F32)
-    vf[pl.ds(far_at, RIM), lip : lip + rows, :] = far_ref[...].astype(F32)
+    vf[pl.ds(near_at, RIM), lip : lip + rows, :] = near_ref[:, 0:rows].astype(F32)
+    vf[pl.ds(far_at, RIM), lip : lip + rows, :] = far_ref[:, 0:rows].astype(F32)
     for at, count, piece in (
-        (RIM, wx, side_ref[0:wx]),
-        (near_at, RIM, side_ref[wx : wx + RIM]),
-        (far_at, RIM, diag_ref[...]),
+        (RIM, wx, side_ref[...]),
+        (near_at, RIM, near_ref[:, rows : rows + lip]),
+        (far_at, RIM, far_ref[:, rows : rows + lip]),
     ):
         piece = piece.astype(F32)
         vf[pl.ds(at, count), 0:lip, :] = jnp.where(iy == 0, 0.0, piece)
@@ -247,18 +247,13 @@
     lip = RIM * cin
     block = volume[0].transpose(1, 2, 0, 3).reshape(wx, wy * cin, wz)
 
-    def rim_y(piece):
-        return jnp.where(low_y, piece[:, -lip:], piece[:, :lip])
-
-    inner = jnp.where(odd_x, block[:RIM], block[-RIM:])
-    outer = jnp.where(odd_x, block[-RIM:], block[:RIM])
+    side = swap(jnp.where(low_y, block[:, -lip:], block[:, :lip]), "sy", 1)
+    both = jnp.concatenate([block, side], axis=1)
+    inner = jnp.where(odd_x, both[:RIM], both[-RIM:])
+    outer = jnp.where(odd_x, both[-RIM:], both[:RIM])
+    pairs = [(i, i + 1) for i in range(1, count_x - 1, 2)]
+    far = lax.ppermute(outer, "sx", pairs + [(j, i) for i, j in pairs])
     near = swap(inner, "sx", 1)
-    pairs = [(i, i + 1) for i in range(1, count_x - 1, 2)]
-    pairs = pairs + [(j, i) for i, j in pairs]
-    far = lax.ppermute(outer, "sx", pairs)
-    crossed = [(2 * i + t, 2 * j + 1 - t) for i, j in pairs for t in range(2)]
-    diag = lax.ppermute(rim_y(outer), ("sx", "sy"), crossed)
-    side = swap(jnp.concatenate([rim_y(block), rim_y(near)], axis=0), "sy", 1)
     cot = cotangent[0].reshape(c2, hx * hy * hz)
 
     body = functools.partial(
@@ -280,7 +275,7 @@
             pltpu.VMEM((8 * c1, lane), BF16),
         ],
         name="local_step",
-    )(*map(near_core, (block, near, far, side, diag)), first_weight, second_weight, near_core(cot))
+    )(*map(near_core, (block, near, far, side, first_weight, second_weight, cot)))
     mine = (keep + swap(send, "sx", 1).astype(F32)).astype(BF16)
     mine = total_over(mine, ("sx", "sy"), [1] + [2 * m for m in bits(count_x)[1:]])
     mine = total_over(mine, ("dp",), bits(lax.axis_size("dp")))

time: 37.3 us -> 35.1 us (0.941)
  starting transfers between devices: 19.4 us -> 16.2 us
  waiting for transfers between devices: 10.7 us -> 12.8 us
  Pallas kernels: 5.09 us -> 4.15 us
    ppermute x10, starting transfers between devices: 17.9 us -> 15.4 us  [swap(): return lax.ppermute(value, axes, [(i, i ^ mask) for i in range(count)])]
    ppermute x10, waiting for transfers between devices: 10.7 us -> 12.8 us  [swap(): return lax.ppermute(value, axes, [(i, i ^ mask) for i in range(count)])]
    pallas_call x1, Pallas kernels: 4.37 us -> 3.43 us  [shards(): pl.pallas_call(body, out_shape=(pltpu.VMEM((c2 // 2, width), F32), pltpu....]
    transpose x1, local copies, waits for them, and re-layouts: 0.02 us -> 0.81 us  [shards(): block = volume[0].transpose(1, 2, 0, 3).reshape(wx, wy * cin, wz)]
    unnamed x4 -> x6, local copies, waits for them, and re-layouts: 0.74 us -> 0.02 us
    ppermute x2 -> x1, starting transfers between devices: 1.46 us -> 0.8 us  [shards(): far = lax.ppermute(outer, 'sx', pairs + [(j, i) for i, j in pairs])]
  transfers between devices with their start and end apart: 12 -> 11, of which waited for: 8 -> 9; matrix products, arithmetic and copies ran while one was open for 1% -> 0% of each run, Pallas kernels for 0% -> 0%
where the time goes in v4:
time: 35.1 us; the launch traced here: 35 us
  starting transfers between devices  16.2 us (46%)
  waiting for transfers between devices  12.8 us (36%)
  Pallas kernels  4.15 us (12%)
  local copies, waits for them, and re-layouts  0.97 us (3%)
  between operations  0.73 us (2%)
    ppermute x10, starting transfers between devices, swap(): return lax.ppermute(value, axes, [(i, i ^ mask) for i in range(count)])  15.4 us
    ppermute x10, waiting for transfers between devices, swap(): return lax.ppermute(value, axes, [(i, i ^ mask) for i in range(count)])  12.8 us
    pallas_call x1, Pallas kernels, shards(): pl.pallas_call(body, out_shape=(pltpu.VMEM((c2 // 2, width), F32), pltpu....  3.43 us
    transpose x1, local copies, waits for them, and re-layouts, shards(): block = volume[0].transpose(1, 2, 0, 3).reshape(wx, wy * cin, wz)  0.81 us
    ppermute x1, starting transfers between devices, shards(): far = lax.ppermute(outer, 'sx', pairs + [(j, i) for i, j in pairs])  0.8 us
    pallas_call x1, Pallas kernels, shards(): pl.pallas_call(functools.partial(join_kernel, g_lane=g_lane), out_shape=(...  0.71 us
  transfers between devices with their start and end apart: 11, of which 9 were waited for; matrix products, arithmetic and copies ran while one was open for 0% of the time, Pallas kernels for 0%

profile of v4, /device:TPU:0, one launch (start us, length us, event | category | flops | bytes accessed | tf_op | source)
XLA Modules:
  0.0 35.0 jit_solution(11389563165950265360)
XLA Ops:
  0.6 0.0 copy-start.2
  0.6 0.8 %copy.6 = bf16[4,8,4,128]{3,2,1,0:T(4,128)(2,1)S(1)} copy(bf16[4,8,4,128]{3,1,0,2:T(8,128)(2,1)} %bitcast.7) | data formatting | bytes 65536 | tf_op jit(solution)/shard_map/transpose | solution.py:248
  1.5 3.0 %collective-permute-start = (bf16[4,12,128]{2,1,0:T(8,128)(2,1)S(1)}, bf16[4,12,128]{2,1,0:T(8,128)(2,1)S(1)}, u32[]{:S(2)}, u32[]{:S(2)}) collective-permute-start(bf16[4,12,128]{2,1,0:T(8,128)(2,1)S(1)} %slice_select_fusion), channel_id=1, source_target_pairs={{0,1},{1,0},{2,3},{3,2},{4,5},{5,4},{6,7},{7,6},{8,9},{9,8},{10,11... | collective-permute-start | bytes 36872 | tf_op jit(solution)/shard_map/ppermute | solution.py:207
  4.5 1.7 %collective-permute-done.side_ref = bf16[4,12,128]{2,1,0:T(8,128)(2,1)S(1)} collective-permute-done((bf16[4,12,128]{2,1,0:T(8,128)(2,1)S(1)}, bf16[4,12,128]{2,1,0:T(8,128)(2,1)S(1)}, u32[]{:S(2)}, u32[]{:S(2)}) %collective-permute-start) | collective-permute-done | bytes 12320 | tf_op jit(solution)/shard_map/ppermute | solution.py:207
  6.3 0.0 copy-start
  6.3 0.8 %collective-permute-start.2 = (bf16[3,44,128]{2,1,0:T(8,128)(2,1)S(1)}, bf16[3,44,128]{2,1,0:T(8,128)(2,1)S(1)}, u32[]{:S(2)}, u32[]{:S(2)}) collective-permute-start(bf16[3,44,128]{2,1,0:T(8,128)(2,1)S(1)} %get-tuple-element.6), channel_id=1, source_target_pairs={{2,4},{4,2},{3,5},{5,3},{10,12},{12,10},{11,13},{13,11},{18,20},{2... | collective-permute-start | bytes 101384 | tf_op jit(solution)/shard_map/ppermute | solution.py:255
  7.1 0.0 copy-start.1
  7.1 3.5 %collective-permute-start.1 = (bf16[3,44,128]{2,1,0:T(8,128)(2,1)S(1)}, bf16[3,44,128]{2,1,0:T(8,128)(2,1)S(1)}, u32[]{:S(2)}, u32[]{:S(2)}) collective-permute-start(bf16[3,44,128]{2,1,0:T(8,128)(2,1)S(1)} %get-tuple-element.7), channel_id=1, source_target_pairs={{0,2},{2,0},{4,6},{6,4},{1,3},{3,1},{5,7},{7,5},{8,10},{10,8},{12,... | collective-permute-start | bytes 101384 | tf_op jit(solution)/shard_map/ppermute | solution.py:207
  10.6 0.0 copy-done.2
  10.6 0.1 reshape_squeeze.3.cot_ref
  10.7 0.0 collective-permute-done.2.far_ref
  10.7 0.7 %collective-permute-done.1.near_ref = bf16[3,44,128]{2,1,0:T(8,128)(2,1)S(1)} collective-permute-done((bf16[3,44,128]{2,1,0:T(8,128)(2,1)S(1)}, bf16[3,44,128]{2,1,0:T(8,128)(2,1)S(1)}, u32[]{:S(2)}, u32[]{:S(2)}) %collective-permute-start.1) | collective-permute-done | bytes 33824 | tf_op jit(solution)/shard_map/ppermute | solution.py:207
  11.4 0.0 copy-done
  11.4 0.0 copy-done.1
  11.4 3.4 %local_step.1 = (f32[32,1024]{1,0:T(8,128)S(1)}, bf16[32,1024]{1,0:T(8,128)(2,1)S(1)}) custom-call(bf16[4,32,128]{2,1,0:T(8,128)(2,1)S(1)} %bitcast.6, bf16[3,44,128]{2,1,0:T(8,128)(2,1)S(1)} %collective-permute-done.1.near_ref, bf16[3,44,128]{2,1,0:T(8,128)(2,1)S(1)} %collective-permute-done.2.far_ref, ...), custom_call_target="tpu_custom_call" | custom-call | tf_op jit(solution)/shard_map/local_step/pallas_call | solution.py:263
  14.9 0.7 %collective-permute-start.3 = (bf16[32,1024]{1,0:T(8,128)(2,1)S(1)}, bf16[32,1024]{1,0:T(8,128)(2,1)S(1)}, u32[]{:S(2)}, u32[]{:S(2)}) collective-permute-start(bf16[32,1024]{1,0:T(8,128)(2,1)S(1)} %get-tuple-element.5), channel_id=1, source_target_pairs={{0,2},{2,0},{4,6},{6,4},{1,3},{3,1},{5,7},{7,5},{8,10},{10,8},{12,... | collective-permute-start | bytes 196616 | tf_op jit(solution)/shard_map/ppermute | solution.py:207
  15.6 0.9 %collective-permute-done.3 = bf16[32,1024]{1,0:T(8,128)(2,1)S(1)} collective-permute-done((bf16[32,1024]{1,0:T(8,128)(2,1)S(1)}, bf16[32,1024]{1,0:T(8,128)(2,1)S(1)}, u32[]{:S(2)}, u32[]{:S(2)}) %collective-permute-start.3) | collective-permute-done | bytes 65568 | tf_op jit(solution)/shard_map/ppermute | solution.py:207
  16.5 3.0 %collective-permute-start.6 = (bf16[32,1024]{1,0:T(8,128)(2,1)S(1)}, bf16[32,1024]{1,0:T(8,128)(2,1)S(1)}, u32[]{:S(2)}, u32[]{:S(2)}) collective-permute-start(bf16[32,1024]{1,0:T(8,128)(2,1)S(1)} %add_convert_fusion.2), channel_id=1, source_target_pairs={{0,5},{1,4},{2,7},{3,6},{4,1},{5,0},{6,3},{7,2},{8,13},{9,12},{10,... | collective-permute-start | bytes 196616 | tf_op jit(solution)/shard_map/ppermute | solution.py:207
  19.5 0.1 collective-permute-start.5
  19.6 0.6 %collective-permute-start.4 = (bf16[32,1024]{1,0:T(8,128)(2,1)S(1)}, bf16[32,1024]{1,0:T(8,128)(2,1)S(1)}, u32[]{:S(2)}, u32[]{:S(2)}) collective-permute-start(bf16[32,1024]{1,0:T(8,128)(2,1)S(1)} %add_convert_fusion.2), channel_id=1, source_target_pairs={{0,1},{1,0},{2,3},{3,2},{4,5},{5,4},{6,7},{7,6},{8,9},{9,8},{10,11... | collective-permute-start | bytes 196616 | tf_op jit(solution)/shard_map/ppermute | solution.py:207
  20.2 1.8 %collective-permute-done.6 = bf16[32,1024]{1,0:T(8,128)(2,1)S(1)} collective-permute-done((bf16[32,1024]{1,0:T(8,128)(2,1)S(1)}, bf16[32,1024]{1,0:T(8,128)(2,1)S(1)}, u32[]{:S(2)}, u32[]{:S(2)}) %collective-permute-start.6) | collective-permute-done | bytes 65568 | tf_op jit(solution)/shard_map/ppermute | solution.py:207
  21.9 1.9 %collective-permute-done.5 = bf16[32,1024]{1,0:T(8,128)(2,1)S(1)} collective-permute-done((bf16[32,1024]{1,0:T(8,128)(2,1)S(1)}, bf16[32,1024]{1,0:T(8,128)(2,1)S(1)}, u32[]{:S(2)}, u32[]{:S(2)}) %collective-permute-start.5) | collective-permute-done | bytes 65568 | tf_op jit(solution)/shard_map/ppermute | solution.py:207
  23.8 0.1 collective-permute-done.4
  23.9 3.7 %collective-permute-start.9 = (bf16[32,1024]{1,0:T(8,128)(2,1)S(1)}, bf16[32,1024]{1,0:T(8,128)(2,1)S(1)}, u32[]{:S(2)}, u32[]{:S(2)}) collective-permute-start(bf16[32,1024]{1,0:T(8,128)(2,1)S(1)} %add_convert_fusion.1), channel_id=1, source_target_pairs={{0,24},{8,16},{16,8},{24,0},{1,25},{9,17},{17,9},{25,1},{2,26},{10... | collective-permute-start | bytes 196616 | tf_op jit(solution)/shard_map/ppermute | solution.py:207
  27.5 0.0 collective-permute-start.8
  27.5 0.8 %collective-permute-start.7 = (bf16[32,1024]{1,0:T(8,128)(2,1)S(1)}, bf16[32,1024]{1,0:T(8,128)(2,1)S(1)}, u32[]{:S(2)}, u32[]{:S(2)}) collective-permute-start(bf16[32,1024]{1,0:T(8,128)(2,1)S(1)} %add_convert_fusion.1), channel_id=1, source_target_pairs={{0,8},{8,0},{16,24},{24,16},{1,9},{9,1},{17,25},{25,17},{2,10},{10... | collective-permute-start | bytes 196616 | tf_op jit(solution)/shard_map/ppermute | solution.py:207
  28.3 1.9 %collective-permute-done.9 = bf16[32,1024]{1,0:T(8,128)(2,1)S(1)} collective-permute-done((bf16[32,1024]{1,0:T(8,128)(2,1)S(1)}, bf16[32,1024]{1,0:T(8,128)(2,1)S(1)}, u32[]{:S(2)}, u32[]{:S(2)}) %collective-permute-start.9) | collective-permute-done | bytes 65568 | tf_op jit(solution)/shard_map/ppermute | solution.py:207
  30.2 2.7 %collective-permute-done.8 = bf16[32,1024]{1,0:T(8,128)(2,1)S(1)} collective-permute-done((bf16[32,1024]{1,0:T(8,128)(2,1)S(1)}, bf16[32,1024]{1,0:T(8,128)(2,1)S(1)}, u32[]{:S(2)}, u32[]{:S(2)}) %collective-permute-start.8) | collective-permute-done | bytes 65568 | tf_op jit(solution)/shard_map/ppermute | solution.py:207
  32.9 0.0 collective-permute-done.7
  32.9 0.1 collective-permute-start.10
  33.0 1.2 %collective-permute-done.10.other_ref = bf16[32,1024]{1,0:T(8,128)(2,1)S(1)} collective-permute-done((bf16[32,1024]{1,0:T(8,128)(2,1)S(1)}, bf16[32,1024]{1,0:T(8,128)(2,1)S(1)}, u32[]{:S(2)}, u32[]{:S(2)}) %collective-permute-start.10) | collective-permute-done | bytes 65568 | tf_op jit(solution)/shard_map/ppermute | solution.py:207
  34.3 0.7 %join.1 = (f32[32,108]{1,0:T(8,128)}, f32[64,864]{1,0:T(8,128)}) custom-call(bf16[32,1024]{1,0:T(8,128)(2,1)S(1)} %add_convert_fusion.mine_ref, bf16[32,1024]{1,0:T(8,128)(2,1)S(1)} %collective-permute-done.10.other_ref), custom_call_target="tpu_custom_call" | custom-call | tf_op jit(solution)/shard_map/join/pallas_call | solution.py:282
  (5 shorter events, 0.1 us)
Async XLA Ops:
  0.6 9.9 %copy-start.2 = (bf16[1,64,2,4,64]{4,3,2,1,0:T(4,128)(2,1)S(1)}, bf16[1,64,2,4,64]{4,3,2,1,0:T(4,128)(2,1)}, u32[]{:S(2)}) copy-start(bf16[1,64,2,4,64]{4,3,2,1,0:T(4,128)(2,1)} %param.7) | copy-start | bytes 196612
  1.5 4.8 %collective-permute-start = (bf16[4,12,128]{2,1,0:T(8,128)(2,1)S(1)}, bf16[4,12,128]{2,1,0:T(8,128)(2,1)S(1)}, u32[]{:S(2)}, u32[]{:S(2)}) collective-permute-start(bf16[4,12,128]{2,1,0:T(8,128)(2,1)S(1)} %slice_select_fusion), channel_id=1, source_target_pairs={{0,1},{1,0},{2,3},{3,2},{4,5},{5,4},{6,7},{7,6},{8,9},{9,8},{10,11... | collective-permute-start | bytes 36872 | tf_op jit(solution)/shard_map/ppermute | solution.py:207
  6.3 5.2 %copy-start = (bf16[64,864]{1,0:T(8,128)(2,1)S(1)}, bf16[64,864]{1,0:T(8,128)(2,1)}, u32[]{:S(2)}) copy-start(bf16[64,864]{1,0:T(8,128)(2,1)} %w2_ref.1) | copy-start | bytes 331780
  6.3 4.4 %collective-permute-start.2 = (bf16[3,44,128]{2,1,0:T(8,128)(2,1)S(1)}, bf16[3,44,128]{2,1,0:T(8,128)(2,1)S(1)}, u32[]{:S(2)}, u32[]{:S(2)}) collective-permute-start(bf16[3,44,128]{2,1,0:T(8,128)(2,1)S(1)} %get-tuple-element.6), channel_id=1, source_target_pairs={{2,4},{4,2},{3,5},{5,3},{10,12},{12,10},{11,13},{13,11},{18,20},{2... | collective-permute-start | bytes 101384 | tf_op jit(solution)/shard_map/ppermute | solution.py:255
  7.1 4.4 %copy-start.1 = (bf16[32,108]{1,0:T(8,128)(2,1)S(1)}, bf16[32,108]{1,0:T(8,128)(2,1)}, u32[]{:S(2)}) copy-start(bf16[32,108]{1,0:T(8,128)(2,1)} %w1_ref.1) | copy-start | bytes 20740
  7.1 4.3 %collective-permute-start.1 = (bf16[3,44,128]{2,1,0:T(8,128)(2,1)S(1)}, bf16[3,44,128]{2,1,0:T(8,128)(2,1)S(1)}, u32[]{:S(2)}, u32[]{:S(2)}) collective-permute-start(bf16[3,44,128]{2,1,0:T(8,128)(2,1)S(1)} %get-tuple-element.7), channel_id=1, source_target_pairs={{0,2},{2,0},{4,6},{6,4},{1,3},{3,1},{5,7},{7,5},{8,10},{10,8},{12,... | collective-permute-start | bytes 101384 | tf_op jit(solution)/shard_map/ppermute | solution.py:207
  14.9 1.7 %collective-permute-start.3 = (bf16[32,1024]{1,0:T(8,128)(2,1)S(1)}, bf16[32,1024]{1,0:T(8,128)(2,1)S(1)}, u32[]{:S(2)}, u32[]{:S(2)}) collective-permute-start(bf16[32,1024]{1,0:T(8,128)(2,1)S(1)} %get-tuple-element.5), channel_id=1, source_target_pairs={{0,2},{2,0},{4,6},{6,4},{1,3},{3,1},{5,7},{7,5},{8,10},{10,8},{12,... | collective-permute-start | bytes 196616 | tf_op jit(solution)/shard_map/ppermute | solution.py:207
  16.5 5.4 %collective-permute-start.6 = (bf16[32,1024]{1,0:T(8,128)(2,1)S(1)}, bf16[32,1024]{1,0:T(8,128)(2,1)S(1)}, u32[]{:S(2)}, u32[]{:S(2)}) collective-permute-start(bf16[32,1024]{1,0:T(8,128)(2,1)S(1)} %add_convert_fusion.2), channel_id=1, source_target_pairs={{0,5},{1,4},{2,7},{3,6},{4,1},{5,0},{6,3},{7,2},{8,13},{9,12},{10,... | collective-permute-start | bytes 196616 | tf_op jit(solution)/shard_map/ppermute | solution.py:207
  19.5 4.3 %collective-permute-start.5 = (bf16[32,1024]{1,0:T(8,128)(2,1)S(1)}, bf16[32,1024]{1,0:T(8,128)(2,1)S(1)}, u32[]{:S(2)}, u32[]{:S(2)}) collective-permute-start(bf16[32,1024]{1,0:T(8,128)(2,1)S(1)} %add_convert_fusion.2), channel_id=1, source_target_pairs={{0,4},{1,5},{2,6},{3,7},{4,0},{5,1},{6,2},{7,3},{8,12},{9,13},{10,... | collective-permute-start | bytes 196616 | tf_op jit(solution)/shard_map/ppermute | solution.py:207
  19.6 4.3 %collective-permute-start.4 = (bf16[32,1024]{1,0:T(8,128)(2,1)S(1)}, bf16[32,1024]{1,0:T(8,128)(2,1)S(1)}, u32[]{:S(2)}, u32[]{:S(2)}) collective-permute-start(bf16[32,1024]{1,0:T(8,128)(2,1)S(1)} %add_convert_fusion.2), channel_id=1, source_target_pairs={{0,1},{1,0},{2,3},{3,2},{4,5},{5,4},{6,7},{7,6},{8,9},{9,8},{10,11... | collective-permute-start | bytes 196616 | tf_op jit(solution)/shard_map/ppermute | solution.py:207
  23.9 6.4 %collective-permute-start.9 = (bf16[32,1024]{1,0:T(8,128)(2,1)S(1)}, bf16[32,1024]{1,0:T(8,128)(2,1)S(1)}, u32[]{:S(2)}, u32[]{:S(2)}) collective-permute-start(bf16[32,1024]{1,0:T(8,128)(2,1)S(1)} %add_convert_fusion.1), channel_id=1, source_target_pairs={{0,24},{8,16},{16,8},{24,0},{1,25},{9,17},{17,9},{25,1},{2,26},{10... | collective-permute-start | bytes 196616 | tf_op jit(solution)/shard_map/ppermute | solution.py:207
  27.5 5.4 %collective-permute-start.8 = (bf16[32,1024]{1,0:T(8,128)(2,1)S(1)}, bf16[32,1024]{1,0:T(8,128)(2,1)S(1)}, u32[]{:S(2)}, u32[]{:S(2)}) collective-permute-start(bf16[32,1024]{1,0:T(8,128)(2,1)S(1)} %add_convert_fusion.1), channel_id=1, source_target_pairs={{0,16},{8,24},{16,0},{24,8},{1,17},{9,25},{17,1},{25,9},{2,18},{10... | collective-permute-start | bytes 196616 | tf_op jit(solution)/shard_map/ppermute | solution.py:207
  27.5 5.4 %collective-permute-start.7 = (bf16[32,1024]{1,0:T(8,128)(2,1)S(1)}, bf16[32,1024]{1,0:T(8,128)(2,1)S(1)}, u32[]{:S(2)}, u32[]{:S(2)}) collective-permute-start(bf16[32,1024]{1,0:T(8,128)(2,1)S(1)} %add_convert_fusion.1), channel_id=1, source_target_pairs={{0,8},{8,0},{16,24},{24,16},{1,9},{9,1},{17,25},{25,17},{2,10},{10... | collective-permute-start | bytes 196616 | tf_op jit(solution)/shard_map/ppermute | solution.py:207
  32.9 1.3 %collective-permute-start.10 = (bf16[32,1024]{1,0:T(8,128)(2,1)S(1)}, bf16[32,1024]{1,0:T(8,128)(2,1)S(1)}, u32[]{:S(2)}, u32[]{:S(2)}) collective-permute-start(bf16[32,1024]{1,0:T(8,128)(2,1)S(1)} %add_convert_fusion.mine_ref), channel_id=1, source_target_pairs={{0,2},{2,0},{4,6},{6,4},{1,3},{3,1},{5,7},{7,5},{8,10},{10,8},{12,... | collective-permute-start | bytes 196616 | tf_op jit(solution)/shard_map/ppermute | solution.py:207

commit v5 on v4

--- a/solution.py
+++ b/solution.py
@@ -23,14 +23,42 @@
     return jnp.where(cond, 1.0, 0.0).astype(BF16)
 
 
+def prepare_kernel(w1_ref, toeplitz_ref, sel_ref, fold_ref, *, cin, hz):
+    lanes = 2 * hz
+    win = 16 * cin
+    ri = lax.broadcasted_iota(jnp.int32, (2 * lanes, 4 * lanes), 0)
+    ci = lax.broadcasted_iota(jnp.int32, (2 * lanes, 4 * lanes), 1)
+    sel_ref[...] = one_hot(
+        ((ri // lanes) == ((ci % lanes) // hz))
+        & ((ri % lanes) == 2 * (ci % hz) + ci // lanes - 1)
+    )
+    wide = w1_ref.shape[1]
+    fi = lax.broadcasted_iota(jnp.int32, (4 * win, wide), 0)
+    ni = lax.broadcasted_iota(jnp.int32, (4 * win, wide), 1)
+    k = ni // cin
+    base = (k % 3) * win + (k // 9) * 4 * cin + ((k // 3) % 3) * cin + ni % cin
+    diff = fi - base
+    folds = [
+        one_hot(diff == fz * win + fx * 4 * cin + fy * cin)
+        for fx in range(2)
+        for fy in range(2)
+        for fz in range(2)
+    ]
+    w1 = w1_ref[...]
+    c1 = w1.shape[0]
+    for s in range(8):
+        fold_ref[s] = folds[s]
+        toeplitz_ref[s * c1 : (s + 1) * c1, :] = mm(w1, folds[s], NT).astype(BF16)
+
+
 def local_kernel(
-    block_ref, near_ref, far_ref, side_ref, w1_ref, w2_ref, cot_ref, keep_ref, send_ref,
+    block_ref, near_ref, far_ref, side_ref, toeplitz_ref, sel_ref, fold_ref, w2_ref, cot_ref, keep_ref, send_ref,
     vf, lhs, s_ref, slope_ref, cols, lower,
     *, cin, hx, hy, hz, g_lane, scale_first, scale_second,
 ):
     nx, ny = hx + 2, hy + 2
     row = ny * hz
-    c1 = w1_ref.shape[0]
+    c1, wide = toeplitz_ref.shape[0] // 8, fold_ref.shape[2]
     win = 16 * cin
     pairs = nx * ny // 2
     lanes = 2 * hz
@@ -53,12 +81,6 @@
         piece = piece.astype(F32)
         vf[pl.ds(at, count), 0:lip, :] = jnp.where(iy == 0, 0.0, piece)
         vf[pl.ds(at, count), lip + rows : 2 * lip + rows, :] = jnp.where(iy == 0, piece, 0.0)
-    ri = lax.broadcasted_iota(jnp.int32, (2 * lanes, 4 * lanes), 0)
-    ci = lax.broadcasted_iota(jnp.int32, (2 * lanes, 4 * lanes), 1)
-    sel = one_hot(
-        ((ri // lanes) == ((ci % lanes) // hz))
-        & ((ri % lanes) == 2 * (ci % hz) + ci // lanes - 1)
-    )
     for p in range(pairs):
         for half in range(2):
             cell = 2 * p + half
@@ -68,27 +90,12 @@
                     p * win + dx * 4 * cin : p * win + (dx + 1) * 4 * cin,
                     half * lanes : (half + 1) * lanes,
                 ] = vf[2 * cx + dx, 2 * cin * cy : 2 * cin * cy + 4 * cin, :].astype(BF16)
-    picked = mm(lhs[...], sel).astype(BF16)
+    picked = mm(lhs[...], sel_ref[...]).astype(BF16)
     for p in range(pairs):
         for o in range(4):
             s_ref[o * win : (o + 1) * win, p * lanes : (p + 1) * lanes] = picked[
                 p * win : (p + 1) * win, o * lanes : (o + 1) * lanes
             ]
-
-    wide = w1_ref.shape[1]
-    fi = lax.broadcasted_iota(jnp.int32, (4 * win, wide), 0)
-    ni = lax.broadcasted_iota(jnp.int32, (4 * win, wide), 1)
-    k = ni // cin
-    base = (k % 3) * win + (k // 9) * 4 * cin + ((k // 3) % 3) * cin + ni % cin
-    diff = fi - base
-    folds = [
-        one_hot(diff == fz * win + fx * 4 * cin + fy * cin)
-        for fx in range(2)
-        for fy in range(2)
-        for fz in range(2)
-    ]
-    w1 = w1_ref[...]
-    toeplitz = jnp.concatenate([mm(w1, f, NT).astype(BF16) for f in folds], axis=0)
 
     lane = lax.broadcasted_iota(jnp.int32, (1, row), 1)
     low_y = jnp.where(iy == 0, hz, 0)
@@ -100,7 +107,7 @@
     own = hy * hz
     for cx in range(nx):
         here = slice(cx * row, (cx + 1) * row)
-        pre = mm(toeplitz, s_ref[:, here])
+        pre = mm(toeplitz_ref[...], s_ref[:, here])
         t = jnp.exp(-jnp.abs(pre))
         r = 1.0 / (1.0 + t)
         soft = jnp.maximum(pre, 0.0) + jnp.log(1.0 + t)
@@ -184,7 +191,7 @@
     first = jnp.zeros((c1, wide), F32)
     for s in range(8):
         part = slice(s * c1, (s + 1) * c1)
-        first = first + mm(high[part], folds[s]) + mm(low[part], folds[s])
+        first = first + mm(high[part], fold_ref[s]) + mm(low[part], fold_ref[s])
     first = first * scale_first
     keep_ref[0:c1, g_lane : g_lane + wide] = jnp.where(is_odd, 0.0, first)
     send_ref[0:c1, g_lane : g_lane + wide] = jnp.where(is_odd, first, 0.0).astype(BF16)
@@ -255,6 +262,19 @@
     far = lax.ppermute(outer, "sx", pairs + [(j, i) for i, j in pairs])
     near = swap(inner, "sx", 1)
     cot = cotangent[0].reshape(c2, hx * hy * hz)
+
+    toeplitz, sel, folds = pl.pallas_call(
+        functools.partial(prepare_kernel, cin=cin, hz=hz),
+        out_shape=(
+            pltpu.VMEM((8 * c1, 4 * win), BF16),
+            pltpu.VMEM((2 * wz, 4 * wz), BF16),
+            pltpu.VMEM((8, 4 * win, wide), BF16),
+        ),
+        cost_estimate=pl.CostEstimate(
+            flops=10**8, bytes_accessed=10**6, transcendentals=0
+        ),
+        name="prepare",
+    )(near_core(first_weight))
 
     body = functools.partial(
         local_kernel, cin=cin, hx=hx, hy=hy, hz=hz, g_lane=g_lane,
@@ -275,7 +295,7 @@
             pltpu.VMEM((8 * c1, lane), BF16),
         ],
         name="local_step",
-    )(*map(near_core, (block, near, far, side, first_weight, second_weight, cot)))
+    )(*map(near_core, (block, near, far, side, toeplitz, sel, folds, second_weight, cot)))
     mine = (keep + swap(send, "sx", 1).astype(F32)).astype(BF16)
     mine = total_over(mine, ("sx", "sy"), [1] + [2 * m for m in bits(count_x)[1:]])
     mine = total_over(mine, ("dp",), bits(lax.axis_size("dp")))

time: 35.1 us -> 34.8 us (level)
  waiting for transfers between devices: 12.8 us -> 12.4 us
    ppermute x10, waiting for transfers between devices: 12.8 us -> 12.4 us  [swap(): return lax.ppermute(value, axes, [(i, i ^ mask) for i in range(count)])]
    pallas_call x0 -> x1, Pallas kernels: none -> 0.43 us  [shards(): pl.pallas_call(functools.partial(prepare_kernel, cin=cin, hz=hz), out_sha...]
  transfers between devices with their start and end apart: 11 -> 11, of which waited for: 9 -> 9; matrix products, arithmetic and copies ran while one was open for 0% -> 0% of each run, Pallas kernels for 0% -> 1%
where the time goes in v5:
time: 34.8 us; the launch traced here: 34.6 us
  starting transfers between devices  15.9 us (46%)
  waiting for transfers between devices  12.4 us (36%)
  Pallas kernels  4.35 us (12%)
  local copies, waits for them, and re-layouts  1.16 us (3%)
  between operations  0.74 us (2%)
    ppermute x10, starting transfers between devices, swap(): return lax.ppermute(value, axes, [(i, i ^ mask) for i in range(count)])  15.2 us
    ppermute x10, waiting for transfers between devices, swap(): return lax.ppermute(value, axes, [(i, i ^ mask) for i in range(count)])  12.4 us
    pallas_call x1, Pallas kernels, shards(): pl.pallas_call(body, out_shape=(pltpu.VMEM((c2 // 2, width), F32), pltpu....  3.2 us
    transpose x1, local copies, waits for them, and re-layouts, shards(): block = volume[0].transpose(1, 2, 0, 3).reshape(wx, wy * cin, wz)  0.81 us
    pallas_call x1, Pallas kernels, shards(): pl.pallas_call(functools.partial(join_kernel, g_lane=g_lane), out_shape=(...  0.71 us
  transfers between devices with their start and end apart: 11, of which 9 were waited for; matrix products, arithmetic and copies ran while one was open for 0% of the time, Pallas kernels for 1%

profile of v5, /device:TPU:0, one launch (start us, length us, event | category | flops | bytes accessed | tf_op | source)
XLA Modules:
  0.0 34.6 jit_solution(12485306930742770245)
XLA Ops:
  0.6 0.0 copy-start.2
  0.6 0.8 %copy.6 = bf16[4,8,4,128]{3,2,1,0:T(4,128)(2,1)S(1)} copy(bf16[4,8,4,128]{3,1,0,2:T(8,128)(2,1)} %bitcast.7) | data formatting | bytes 65536 | tf_op jit(solution)/shard_map/transpose | solution.py:255
  1.5 3.0 %collective-permute-start = (bf16[4,12,128]{2,1,0:T(8,128)(2,1)S(1)}, bf16[4,12,128]{2,1,0:T(8,128)(2,1)S(1)}, u32[]{:S(2)}, u32[]{:S(2)}) collective-permute-start(bf16[4,12,128]{2,1,0:T(8,128)(2,1)S(1)} %slice_select_fusion), channel_id=1, source_target_pairs={{0,1},{1,0},{2,3},{3,2},{4,5},{5,4},{6,7},{7,6},{8,9},{9,8},{10,11... | collective-permute-start | bytes 36872 | tf_op jit(solution)/shard_map/ppermute | solution.py:214
  4.5 1.7 %collective-permute-done.side_ref = bf16[4,12,128]{2,1,0:T(8,128)(2,1)S(1)} collective-permute-done((bf16[4,12,128]{2,1,0:T(8,128)(2,1)S(1)}, bf16[4,12,128]{2,1,0:T(8,128)(2,1)S(1)}, u32[]{:S(2)}, u32[]{:S(2)}) %collective-permute-start) | collective-permute-done | bytes 12320 | tf_op jit(solution)/shard_map/ppermute | solution.py:214
  6.3 0.7 %collective-permute-start.2 = (bf16[3,44,128]{2,1,0:T(8,128)(2,1)S(1)}, bf16[3,44,128]{2,1,0:T(8,128)(2,1)S(1)}, u32[]{:S(2)}, u32[]{:S(2)}) collective-permute-start(bf16[3,44,128]{2,1,0:T(8,128)(2,1)S(1)} %get-tuple-element.12), channel_id=1, source_target_pairs={{2,4},{4,2},{3,5},{5,3},{10,12},{12,10},{11,13},{13,11},{18,20},{2... | collective-permute-start | bytes 101384 | tf_op jit(solution)/shard_map/ppermute | solution.py:262
  6.9 0.0 copy-start.1
  6.9 3.5 %collective-permute-start.1 = (bf16[3,44,128]{2,1,0:T(8,128)(2,1)S(1)}, bf16[3,44,128]{2,1,0:T(8,128)(2,1)S(1)}, u32[]{:S(2)}, u32[]{:S(2)}) collective-permute-start(bf16[3,44,128]{2,1,0:T(8,128)(2,1)S(1)} %get-tuple-element.13), channel_id=1, source_target_pairs={{0,2},{2,0},{4,6},{6,4},{1,3},{3,1},{5,7},{7,5},{8,10},{10,8},{12,... | collective-permute-start | bytes 101384 | tf_op jit(solution)/shard_map/ppermute | solution.py:214
  10.4 0.0 copy-done.2
  10.4 0.1 reshape_squeeze.3.cot_ref
  10.6 0.0 copy-done.1
  10.6 0.0 copy-start
  10.6 0.4 %prepare.1 = (bf16[256,256]{1,0:T(8,128)(2,1)S(1)}, bf16[256,512]{1,0:T(8,128)(2,1)S(1)}, bf16[8,256,108]{2,1,0:T(8,128)(2,1)S(1)}) custom-call(bf16[32,108]{1,0:T(8,128)(2,1)S(1)} %copy-done.1), custom_call_target="tpu_custom_call" | custom-call | flops 100000000 | bytes 1000000 | tf_op jit(solution)/shard_map/prepare/pallas_call | solution.py:266
  11.0 0.0 collective-permute-done.2.far_ref
  11.0 0.2 collective-permute-done.1.near_ref
  11.3 0.2 copy-done
  11.5 3.2 %local_step.1 = (f32[32,1024]{1,0:T(8,128)S(1)}, bf16[32,1024]{1,0:T(8,128)(2,1)S(1)}) custom-call(bf16[4,32,128]{2,1,0:T(8,128)(2,1)S(1)} %bitcast.6, bf16[3,44,128]{2,1,0:T(8,128)(2,1)S(1)} %collective-permute-done.1.near_ref, bf16[3,44,128]{2,1,0:T(8,128)(2,1)S(1)} %collective-permute-done.2.far_ref, ...), custom_call_target="tpu_custom_call" | custom-call | tf_op jit(solution)/shard_map/local_step/pallas_call | solution.py:283
  14.7 0.6 %collective-permute-start.3 = (bf16[32,1024]{1,0:T(8,128)(2,1)S(1)}, bf16[32,1024]{1,0:T(8,128)(2,1)S(1)}, u32[]{:S(2)}, u32[]{:S(2)}) collective-permute-start(bf16[32,1024]{1,0:T(8,128)(2,1)S(1)} %get-tuple-element.11), channel_id=1, source_target_pairs={{0,2},{2,0},{4,6},{6,4},{1,3},{3,1},{5,7},{7,5},{8,10},{10,8},{12,... | collective-permute-start | bytes 196616 | tf_op jit(solution)/shard_map/ppermute | solution.py:214
  15.2 0.9 %collective-permute-done.3 = bf16[32,1024]{1,0:T(8,128)(2,1)S(1)} collective-permute-done((bf16[32,1024]{1,0:T(8,128)(2,1)S(1)}, bf16[32,1024]{1,0:T(8,128)(2,1)S(1)}, u32[]{:S(2)}, u32[]{:S(2)}) %collective-permute-start.3) | collective-permute-done | bytes 65568 | tf_op jit(solution)/shard_map/ppermute | solution.py:214
  16.2 3.0 %collective-permute-start.6 = (bf16[32,1024]{1,0:T(8,128)(2,1)S(1)}, bf16[32,1024]{1,0:T(8,128)(2,1)S(1)}, u32[]{:S(2)}, u32[]{:S(2)}) collective-permute-start(bf16[32,1024]{1,0:T(8,128)(2,1)S(1)} %add_convert_fusion.2), channel_id=1, source_target_pairs={{0,5},{1,4},{2,7},{3,6},{4,1},{5,0},{6,3},{7,2},{8,13},{9,12},{10,... | collective-permute-start | bytes 196616 | tf_op jit(solution)/shard_map/ppermute | solution.py:214
  19.1 0.1 collective-permute-start.5
  19.2 0.6 %collective-permute-start.4 = (bf16[32,1024]{1,0:T(8,128)(2,1)S(1)}, bf16[32,1024]{1,0:T(8,128)(2,1)S(1)}, u32[]{:S(2)}, u32[]{:S(2)}) collective-permute-start(bf16[32,1024]{1,0:T(8,128)(2,1)S(1)} %add_convert_fusion.2), channel_id=1, source_target_pairs={{0,1},{1,0},{2,3},{3,2},{4,5},{5,4},{6,7},{7,6},{8,9},{9,8},{10,11... | collective-permute-start | bytes 196616 | tf_op jit(solution)/shard_map/ppermute | solution.py:214
  19.8 1.8 %collective-permute-done.6 = bf16[32,1024]{1,0:T(8,128)(2,1)S(1)} collective-permute-done((bf16[32,1024]{1,0:T(8,128)(2,1)S(1)}, bf16[32,1024]{1,0:T(8,128)(2,1)S(1)}, u32[]{:S(2)}, u32[]{:S(2)}) %collective-permute-start.6) | collective-permute-done | bytes 65568 | tf_op jit(solution)/shard_map/ppermute | solution.py:214
  21.6 1.9 %collective-permute-done.5 = bf16[32,1024]{1,0:T(8,128)(2,1)S(1)} collective-permute-done((bf16[32,1024]{1,0:T(8,128)(2,1)S(1)}, bf16[32,1024]{1,0:T(8,128)(2,1)S(1)}, u32[]{:S(2)}, u32[]{:S(2)}) %collective-permute-start.5) | collective-permute-done | bytes 65568 | tf_op jit(solution)/shard_map/ppermute | solution.py:214
  23.4 0.1 collective-permute-done.4
  23.5 3.7 %collective-permute-start.9 = (bf16[32,1024]{1,0:T(8,128)(2,1)S(1)}, bf16[32,1024]{1,0:T(8,128)(2,1)S(1)}, u32[]{:S(2)}, u32[]{:S(2)}) collective-permute-start(bf16[32,1024]{1,0:T(8,128)(2,1)S(1)} %add_convert_fusion.1), channel_id=1, source_target_pairs={{0,24},{8,16},{16,8},{24,0},{1,25},{9,17},{17,9},{25,1},{2,26},{10... | collective-permute-start | bytes 196616 | tf_op jit(solution)/shard_map/ppermute | solution.py:214
  27.2 0.0 collective-permute-start.8
  27.2 0.8 %collective-permute-start.7 = (bf16[32,1024]{1,0:T(8,128)(2,1)S(1)}, bf16[32,1024]{1,0:T(8,128)(2,1)S(1)}, u32[]{:S(2)}, u32[]{:S(2)}) collective-permute-start(bf16[32,1024]{1,0:T(8,128)(2,1)S(1)} %add_convert_fusion.1), channel_id=1, source_target_pairs={{0,8},{8,0},{16,24},{24,16},{1,9},{9,1},{17,25},{25,17},{2,10},{10... | collective-permute-start | bytes 196616 | tf_op jit(solution)/shard_map/ppermute | solution.py:214
  28.0 1.9 %collective-permute-done.9 = bf16[32,1024]{1,0:T(8,128)(2,1)S(1)} collective-permute-done((bf16[32,1024]{1,0:T(8,128)(2,1)S(1)}, bf16[32,1024]{1,0:T(8,128)(2,1)S(1)}, u32[]{:S(2)}, u32[]{:S(2)}) %collective-permute-start.9) | collective-permute-done | bytes 65568 | tf_op jit(solution)/shard_map/ppermute | solution.py:214
  29.9 2.7 %collective-permute-done.8 = bf16[32,1024]{1,0:T(8,128)(2,1)S(1)} collective-permute-done((bf16[32,1024]{1,0:T(8,128)(2,1)S(1)}, bf16[32,1024]{1,0:T(8,128)(2,1)S(1)}, u32[]{:S(2)}, u32[]{:S(2)}) %collective-permute-start.8) | collective-permute-done | bytes 65568 | tf_op jit(solution)/shard_map/ppermute | solution.py:214
  32.5 0.0 collective-permute-done.7
  32.6 0.1 collective-permute-start.10
  32.7 1.2 %collective-permute-done.10.other_ref = bf16[32,1024]{1,0:T(8,128)(2,1)S(1)} collective-permute-done((bf16[32,1024]{1,0:T(8,128)(2,1)S(1)}, bf16[32,1024]{1,0:T(8,128)(2,1)S(1)}, u32[]{:S(2)}, u32[]{:S(2)}) %collective-permute-start.10) | collective-permute-done | bytes 65568 | tf_op jit(solution)/shard_map/ppermute | solution.py:214
  33.9 0.7 %join.1 = (f32[32,108]{1,0:T(8,128)}, f32[64,864]{1,0:T(8,128)}) custom-call(bf16[32,1024]{1,0:T(8,128)(2,1)S(1)} %add_convert_fusion.mine_ref, bf16[32,1024]{1,0:T(8,128)(2,1)S(1)} %collective-permute-done.10.other_ref), custom_call_target="tpu_custom_call" | custom-call | tf_op jit(solution)/shard_map/join/pallas_call | solution.py:302
  (5 shorter events, 0.1 us)
Async XLA Ops:
  0.6 9.8 %copy-start.2 = (bf16[1,64,2,4,64]{4,3,2,1,0:T(4,128)(2,1)S(1)}, bf16[1,64,2,4,64]{4,3,2,1,0:T(4,128)(2,1)}, u32[]{:S(2)}) copy-start(bf16[1,64,2,4,64]{4,3,2,1,0:T(4,128)(2,1)} %param.7) | copy-start | bytes 196612
  1.5 4.8 %collective-permute-start = (bf16[4,12,128]{2,1,0:T(8,128)(2,1)S(1)}, bf16[4,12,128]{2,1,0:T(8,128)(2,1)S(1)}, u32[]{:S(2)}, u32[]{:S(2)}) collective-permute-start(bf16[4,12,128]{2,1,0:T(8,128)(2,1)S(1)} %slice_select_fusion), channel_id=1, source_target_pairs={{0,1},{1,0},{2,3},{3,2},{4,5},{5,4},{6,7},{7,6},{8,9},{9,8},{10,11... | collective-permute-start | bytes 36872 | tf_op jit(solution)/shard_map/ppermute | solution.py:214
  6.3 4.8 %collective-permute-start.2 = (bf16[3,44,128]{2,1,0:T(8,128)(2,1)S(1)}, bf16[3,44,128]{2,1,0:T(8,128)(2,1)S(1)}, u32[]{:S(2)}, u32[]{:S(2)}) collective-permute-start(bf16[3,44,128]{2,1,0:T(8,128)(2,1)S(1)} %get-tuple-element.12), channel_id=1, source_target_pairs={{2,4},{4,2},{3,5},{5,3},{10,12},{12,10},{11,13},{13,11},{18,20},{2... | collective-permute-start | bytes 101384 | tf_op jit(solution)/shard_map/ppermute | solution.py:262
  6.9 3.6 %copy-start.1 = (bf16[32,108]{1,0:T(8,128)(2,1)S(1)}, bf16[32,108]{1,0:T(8,128)(2,1)}, u32[]{:S(2)}) copy-start(bf16[32,108]{1,0:T(8,128)(2,1)} %w1_ref.1) | copy-start | bytes 20740
  6.9 4.3 %collective-permute-start.1 = (bf16[3,44,128]{2,1,0:T(8,128)(2,1)S(1)}, bf16[3,44,128]{2,1,0:T(8,128)(2,1)S(1)}, u32[]{:S(2)}, u32[]{:S(2)}) collective-permute-start(bf16[3,44,128]{2,1,0:T(8,128)(2,1)S(1)} %get-tuple-element.13), channel_id=1, source_target_pairs={{0,2},{2,0},{4,6},{6,4},{1,3},{3,1},{5,7},{7,5},{8,10},{10,8},{12,... | collective-permute-start | bytes 101384 | tf_op jit(solution)/shard_map/ppermute | solution.py:214
  10.6 0.9 %copy-start = (bf16[64,864]{1,0:T(8,128)(2,1)S(1)}, bf16[64,864]{1,0:T(8,128)(2,1)}, u32[]{:S(2)}) copy-start(bf16[64,864]{1,0:T(8,128)(2,1)} %w2_ref.1) | copy-start | bytes 331780
  14.7 1.5 %collective-permute-start.3 = (bf16[32,1024]{1,0:T(8,128)(2,1)S(1)}, bf16[32,1024]{1,0:T(8,128)(2,1)S(1)}, u32[]{:S(2)}, u32[]{:S(2)}) collective-permute-start(bf16[32,1024]{1,0:T(8,128)(2,1)S(1)} %get-tuple-element.11), channel_id=1, source_target_pairs={{0,2},{2,0},{4,6},{6,4},{1,3},{3,1},{5,7},{7,5},{8,10},{10,8},{12,... | collective-permute-start | bytes 196616 | tf_op jit(solution)/shard_map/ppermute | solution.py:214
  16.2 5.4 %collective-permute-start.6 = (bf16[32,1024]{1,0:T(8,128)(2,1)S(1)}, bf16[32,1024]{1,0:T(8,128)(2,1)S(1)}, u32[]{:S(2)}, u32[]{:S(2)}) collective-permute-start(bf16[32,1024]{1,0:T(8,128)(2,1)S(1)} %add_convert_fusion.2), channel_id=1, source_target_pairs={{0,5},{1,4},{2,7},{3,6},{4,1},{5,0},{6,3},{7,2},{8,13},{9,12},{10,... | collective-permute-start | bytes 196616 | tf_op jit(solution)/shard_map/ppermute | solution.py:214
  19.1 4.3 %collective-permute-start.5 = (bf16[32,1024]{1,0:T(8,128)(2,1)S(1)}, bf16[32,1024]{1,0:T(8,128)(2,1)S(1)}, u32[]{:S(2)}, u32[]{:S(2)}) collective-permute-start(bf16[32,1024]{1,0:T(8,128)(2,1)S(1)} %add_convert_fusion.2), channel_id=1, source_target_pairs={{0,4},{1,5},{2,6},{3,7},{4,0},{5,1},{6,2},{7,3},{8,12},{9,13},{10,... | collective-permute-start | bytes 196616 | tf_op jit(solution)/shard_map/ppermute | solution.py:214
  19.2 4.3 %collective-permute-start.4 = (bf16[32,1024]{1,0:T(8,128)(2,1)S(1)}, bf16[32,1024]{1,0:T(8,128)(2,1)S(1)}, u32[]{:S(2)}, u32[]{:S(2)}) collective-permute-start(bf16[32,1024]{1,0:T(8,128)(2,1)S(1)} %add_convert_fusion.2), channel_id=1, source_target_pairs={{0,1},{1,0},{2,3},{3,2},{4,5},{5,4},{6,7},{7,6},{8,9},{9,8},{10,11... | collective-permute-start | bytes 196616 | tf_op jit(solution)/shard_map/ppermute | solution.py:214
  23.5 6.4 %collective-permute-start.9 = (bf16[32,1024]{1,0:T(8,128)(2,1)S(1)}, bf16[32,1024]{1,0:T(8,128)(2,1)S(1)}, u32[]{:S(2)}, u32[]{:S(2)}) collective-permute-start(bf16[32,1024]{1,0:T(8,128)(2,1)S(1)} %add_convert_fusion.1), channel_id=1, source_target_pairs={{0,24},{8,16},{16,8},{24,0},{1,25},{9,17},{17,9},{25,1},{2,26},{10... | collective-permute-start | bytes 196616 | tf_op jit(solution)/shard_map/ppermute | solution.py:214
  27.2 5.4 %collective-permute-start.8 = (bf16[32,1024]{1,0:T(8,128)(2,1)S(1)}, bf16[32,1024]{1,0:T(8,128)(2,1)S(1)}, u32[]{:S(2)}, u32[]{:S(2)}) collective-permute-start(bf16[32,1024]{1,0:T(8,128)(2,1)S(1)} %add_convert_fusion.1), channel_id=1, source_target_pairs={{0,16},{8,24},{16,0},{24,8},{1,17},{9,25},{17,1},{25,9},{2,18},{10... | collective-permute-start | bytes 196616 | tf_op jit(solution)/shard_map/ppermute | solution.py:214
  27.2 5.4 %collective-permute-start.7 = (bf16[32,1024]{1,0:T(8,128)(2,1)S(1)}, bf16[32,1024]{1,0:T(8,128)(2,1)S(1)}, u32[]{:S(2)}, u32[]{:S(2)}) collective-permute-start(bf16[32,1024]{1,0:T(8,128)(2,1)S(1)} %add_convert_fusion.1), channel_id=1, source_target_pairs={{0,8},{8,0},{16,24},{24,16},{1,9},{9,1},{17,25},{25,17},{2,10},{10... | collective-permute-start | bytes 196616 | tf_op jit(solution)/shard_map/ppermute | solution.py:214
  32.6 1.3 %collective-permute-start.10 = (bf16[32,1024]{1,0:T(8,128)(2,1)S(1)}, bf16[32,1024]{1,0:T(8,128)(2,1)S(1)}, u32[]{:S(2)}, u32[]{:S(2)}) collective-permute-start(bf16[32,1024]{1,0:T(8,128)(2,1)S(1)} %add_convert_fusion.mine_ref), channel_id=1, source_target_pairs={{0,2},{2,0},{4,6},{6,4},{1,3},{3,1},{5,7},{7,5},{8,10},{10,8},{12,... | collective-permute-start | bytes 196616 | tf_op jit(solution)/shard_map/ppermute | solution.py:214
